TPU v7x, 256 devices: a whole 4x4x8 slice. The times are simulated.
256 devices in a mesh: dp: 16 (over z, y_lo), mp: 16 (over y_hi, x, core).
Axes of the slice: x: 4, y: 4 (y_hi: 2, y_lo: 2; y = y_hi * 2 + y_lo), z: 8, core: 2. Of those that a mesh axis runs over, the one named last changes fastest.
Arguments:
- gradient: bfloat16 [1, 4096, 4096], P(None, 'mp', 'dp'), may hold values from -6 to 6
- first_moment: float32 [1, 4096, 4096], P(None, 'mp', 'dp'), may hold values from -3 to 3
- second_moment: float32 [1, 4096, 4096], P(None, 'mp', 'dp'), may hold values from 0.0625 to 1
- left_factor: float32 [1, 4096, 4096], P(None, 'mp', 'dp'), may hold values from -18 to 18
- right_factor: float32 [1, 4096, 4096], P(None, 'mp', 'dp'), may hold values from -18 to 18
- left_basis: bfloat16 [1, 4096, 4096], P(None, 'dp', 'mp'), may hold values from -0.09375 to 0.09375
- right_basis: bfloat16 [1, 4096, 4096], P(None, 'mp', 'dp'), may hold values from -0.09375 to 0.09375
Outputs:
- new_first_moment: float32 [1, 4096, 4096], P(None, 'mp', 'dp')
- new_second_moment: float32 [1, 4096, 4096], P(None, 'mp', 'dp')
- new_left_factor: float32 [1, 4096, 4096], P(None, 'mp', 'dp')
- new_right_factor: float32 [1, 4096, 4096], P(None, 'mp', 'dp')
- update: bfloat16 [1, 4096, 4096], P(None, 'mp', 'dp')
All inputs are finite; a program needn't handle non-finite values.
Results may differ from a plain program's by a relative error of at most 0.014.
Values may be sent and summed in bfloat16 or wider, within the bound.
No kernel may reach another device: no remote copies, remote signals or barrier semaphores. Data moves between devices by JAX's collectives and lax.ppermute only.
A program may use at most 64 MiB of HBM per device.

v0:
```python
import jax
import jax.numpy as jnp
from jax import lax
from jax.experimental import pallas as pl
from jax.experimental.pallas import tpu as pltpu
from jax.sharding import PartitionSpec as P


decay_moment = 0.95
decay_factor = 0.95
epsilon = 1e-08


N = 8
SIDE = 256
bf16, f32 = jnp.bfloat16, jnp.float32

TN = (((0,), (0,)), ((), ()))
NN = (((1,), (0,)), ((), ()))
NT = (((1,), (1,)), ((), ()))


def around(i, t):
    return (((i >> 2) + (t >> 2)) & 1) * 4 + ((i + t) & 3)


def back(i, t):
    return (((i >> 2) - (t >> 2)) & 1) * 4 + ((i - t) & 3)


def along_z(x, s):
    return lax.ppermute(x, "dp", [(d, (d + 2 * s) % 16) for d in range(16)])


def other_core(x):
    return lax.ppermute(x, "mp", [(m, m ^ 1) for m in range(16)])


def neighbour(x):
    return lax.ppermute(x, "dp", [(d, d ^ 1) for d in range(16)])


def mixed(x, place):
    pairs = []
    for d in range(16):
        for m in range(16):
            y, c = place(d & 1, m & 1)
            pairs.append((((d & ~1) | y) * 16 + ((m & ~1) | c), d * 16 + m))
    return lax.ppermute(x, ("dp", "mp"), pairs)


def to_swapped(x, t):
    pairs = []
    for d in range(16):
        for m in range(16):
            to_d = (d & ~1) | (m & 1)
            to_m = 2 * around(m >> 1, t) + (d & 1)
            pairs.append((d * 16 + m, to_d * 16 + to_m))
    return lax.ppermute(x, ("dp", "mp"), pairs)


Z_GROUPS = [[2 * z + y for z in range(N)] for y in range(2)]
PLANE_GROUPS = [[2 * i + c for i in range(N)] for c in range(2)]


def exchange(x, axis, groups):
    return lax.all_to_all(x, axis, 0, 0, axis_index_groups=groups, tiled=True)


def exchange_z(x):
    return exchange(x, "dp", Z_GROUPS)


def exchange_plane(x):
    return exchange(x, "mp", PLANE_GROUPS)


def everywhere_z(x):
    return exchange_z(jnp.broadcast_to(x, (N, *x.shape)))


def gather_z(x):
    return [x] + [along_z(x, s) for s in range(1, N)]


def dot(a, b, dims):
    return lax.dot_general(a, b, dims, preferred_element_type=f32)


def z_back(at, s):
    return (at[0] - s) & 7


def z_on(at, s):
    return (at[0] + s) & 7


def plane_back(at, t):
    return back(at[1], t)


def plane_on(at, t):
    return around(at[1], t)


BLOCK = jax.ShapeDtypeStruct((SIDE, SIDE), bf16)
WIDE = jax.ShapeDtypeStruct((SIDE, SIDE), f32)
PANEL = jax.ShapeDtypeStruct((N, SIDE, SIDE), bf16)


def call(body, at, operands, outs, scratch=(), products=0):
    vmem = pl.BlockSpec(memory_space=pltpu.VMEM)
    moved = sum(o.size * o.dtype.itemsize for o in (*operands, *outs))
    return pl.pallas_call(
        body,
        out_shape=outs,
        in_specs=[pl.BlockSpec(memory_space=pltpu.SMEM)] + [vmem] * len(operands),
        out_specs=[vmem] * len(outs),
        scratch_shapes=list(scratch),
        cost_estimate=pl.CostEstimate(
            flops=products * 2 * SIDE**3, bytes_accessed=moved, transcendentals=0
        ),
    )(at, *operands)


def pack(at, blocks):
    def body(at, *refs):
        for t in range(N):
            refs[N][plane_back(at, t)] = refs[t][...]

    return call(body, at, blocks, [PANEL])[0]


def contract(at, blocks, own, other, dims):
    def body(at, blocks, own, other, keep, send):
        if dims == TN:
            left = blocks[...].reshape(N * SIDE, SIDE)
        else:
            left = jnp.concatenate([blocks[j] for j in range(N)], axis=1)
        one = dot(left, own[...].reshape(N * SIDE, SIDE), dims)
        two = dot(left, other[...].reshape(N * SIDE, SIDE), dims)
        same = at[2] == at[3]
        keep[...] = jnp.where(same, one, two)
        send[...] = jnp.where(same, two, one).astype(bf16)

    return call(body, at, [blocks, own, other], [WIDE, BLOCK], (), 2 * N)


def ordered(at, mine, beside, axis):
    same = at[2] == at[3]
    one = jnp.where(same, mine[...], beside[...])
    two = jnp.where(same, beside[...], mine[...])
    return jnp.concatenate([one, two], axis=axis)


def spread(at, mine, beside, own, other, apart=False):
    def body(at, mine, beside, own, other, *rest):
        both = ordered(at, mine, beside, 1)
        held = rest[-1]

        @pl.loop(0, N, step=2)
        def _(j):
            two = pl.ds(j, 2)
            right = jnp.concatenate(
                [own[two].reshape(2 * SIDE, SIDE), other[two].reshape(2 * SIDE, SIDE)], axis=1
            )
            pair = dot(both, right, NT).astype(held.dtype)
            held[j] = pair[:, :SIDE]
            held[j + 1] = pair[:, SIDE:]

        if apart:
            rest[0][...] = held[z_on(at, 0)]
            for s in range(1, N):
                rest[s][...] = held[z_on(at, s)].astype(bf16)

    outs = [WIDE] + [BLOCK] * (N - 1) if apart else [PANEL]
    scratch = [pltpu.VMEM((N, SIDE, SIDE), f32)] if apart else []
    return call(body, at, [mine, beside, own, other], outs, scratch, 2 * N)


def rotate_back(at, first, second, mine, beside):
    def body(at, first, second, mine, beside, out):
        both = ordered(at, mine, beside, 0)

        @pl.loop(0, N, step=2)
        def _(j):
            two = pl.ds(j, 2)
            left = jnp.concatenate(
                [first[two].reshape(2 * SIDE, SIDE), second[two].reshape(2 * SIDE, SIDE)], axis=1
            )
            out[two] = dot(left, both, NN).astype(bf16).reshape(2, SIDE, SIDE)

    return call(body, at, [first, second, mine, beside], [PANEL], (), 2 * N)[0]


def right_terms(at, blocks, mine, beside):
    def body(at, *refs):
        parts, (mine, beside), rest = refs[:N], refs[N : N + 2], refs[N + 2 :]
        keep, send, panel = rest
        both = ordered(at, mine, beside, 1)
        for s in range(N):
            panel[z_back(at, s)] = parts[s][...]

        @pl.loop(0, N)
        def _(j):
            term = dot(panel[j], both, TN).astype(bf16)
            keep[j] = term[:, :SIDE]
            send[j] = term[:, SIDE:]

    scratch = [pltpu.VMEM((N, SIDE, SIDE), bf16)]
    return call(body, at, [*blocks, mine, beside], [PANEL, PANEL], scratch, 2 * N)


def chip_sum(at, mine, arrived):
    def body(at, mine, arrived, *sends):
        for t in range(N):
            j = plane_on(at, t)
            sends[t][...] = (mine[j].astype(f32) + arrived[j].astype(f32)).astype(bf16)

    return call(body, at, [mine, arrived], [BLOCK] * N)


def summed(keep, arrived):
    total = keep
    for a in arrived:
        total = total + a.astype(f32)
    return total


def update_step(
    gradient, first_moment, second_moment, left_factor, right_factor, left_basis, right_basis
):
    scale = 1.0 - decay_factor
    g, left, right = gradient[0], left_basis[0], right_basis[0]
    d, m = lax.axis_index("dp"), lax.axis_index("mp")
    at = jnp.stack([d >> 1, m >> 1, m & 1, d & 1]).astype(jnp.int32)

    left_panel = everywhere_z(left)
    arrived = [to_swapped(g, t) for t in range(N)]
    g_own = pack(at, arrived)
    r_block = to_swapped(right, 0)
    r_own = exchange_plane(jnp.broadcast_to(r_block, (N, SIDE, SIDE)))
    g_other = other_core(g_own)
    r_other = other_core(r_own)
    g_beside = neighbour(g)

    keep, send = contract(at, left_panel, g_own, g_other, TN)
    turned = neighbour(send)
    rotated_left = (keep + turned.astype(f32)).astype(bf16)
    rotated_left = everywhere_z(rotated_left)
    keep, send = contract(at, rotated_left, r_own, r_other, NN)
    turned = neighbour(send)
    rotated = keep + turned.astype(f32)

    new_first = decay_moment * first_moment[0] + (1.0 - decay_moment) * rotated
    new_second = decay_moment * second_moment[0] + (1.0 - decay_moment) * rotated * rotated
    direction = (new_first / (jnp.sqrt(new_second) + epsilon)).astype(bf16)

    first = mixed(left_panel, lambda y, c: (c, y))
    second = mixed(left_panel, lambda y, c: (c, 1 - y))
    direction_beside = other_core(direction)
    terms = rotate_back(at, first, second, direction, direction_beside)
    terms = exchange_plane(terms)
    back_left = jnp.sum(terms, axis=0, dtype=f32).astype(bf16)
    back_beside = neighbour(back_left)
    terms = spread(at, back_left, back_beside, r_own, r_other)[0]
    terms = exchange_z(terms)
    update = jnp.sum(terms, axis=0, dtype=f32).astype(bf16)

    keep, *sends = spread(at, g, g_beside, g_own, g_other, True)
    arrived = [along_z(b, s + 1) for s, b in enumerate(sends)]
    new_left = decay_factor * left_factor[0] + scale * summed(keep, arrived)

    row = gather_z(g)
    mine, theirs = right_terms(at, row, g, g_beside)
    theirs = other_core(theirs)
    sends = chip_sum(at, mine, theirs)
    arrived = [to_swapped(b, t) for t, b in enumerate(sends)]
    new_right = decay_factor * right_factor[0] + scale * summed(0.0, arrived)
    return tuple(x[None] for x in (new_first, new_second, new_left, new_right, update))


def solution(mesh):
    in_specs = (P(None, "mp", "dp"),) * 5 + (P(None, "dp", "mp"), P(None, "mp", "dp"))
    out_specs = (P(None, "mp", "dp"),) * 5
    return jax.shard_map(
        update_step, mesh=mesh, in_specs=in_specs, out_specs=out_specs, check_vma=False
    )
```

profile of v0, /device:TPU:16, one launch (start us, length us, event | category | flops | bytes accessed | tf_op | source)
XLA Modules:
  0.0 251.0 jit_solution(47524866239841290)
XLA Ops:
  0.6 2.0 broadcast_in_dim.24
  2.6 8.6 %all-to-all-start = ((bf16[8,256,256]{2,1,0:T(8,128)(2,1)}), bf16[8,256,256]{2,1,0:T(8,128)(2,1)S(1)}, u32[]{:S(2)}, u32[]{:S(2)}) async-start(bf16[8,256,256]{2,1,0:T(8,128)(2,1)} %broadcast_in_dim.24), calls=%async_computation | async-start | bytes 2097152 | tf_op jit(solution)/shard_map/all_to_all | solution.py:67
  11.9 1.6 collective-permute-start.1
  13.4 2.7 %collective-permute-start.2 = (bf16[256,256]{1,0:T(8,128)(2,1)S(1)}, bf16[256,256]{1,0:T(8,128)(2,1)S(1)}, u32[]{:S(2)}, u32[]{:S(2)}) collective-permute-start(bf16[256,256]{1,0:T(8,128)(2,1)S(1)} %bitcast.42), channel_id=1, source_target_pairs={{0,4},{1,20},{2,6},{3,22},{4,0},{5,16},{6,2},{7,18},{8,12},{9,28},... | collective-permute-start | bytes 393224 | tf_op jit(solution)/shard_map/ppermute | solution.py:59
  16.2 1.4 collective-permute-start.3
  18.0 3.2 %collective-permute-start.5 = (bf16[256,256]{1,0:T(8,128)(2,1)S(1)}, bf16[256,256]{1,0:T(8,128)(2,1)S(1)}, u32[]{:S(2)}, u32[]{:S(2)}) collective-permute-start(bf16[256,256]{1,0:T(8,128)(2,1)S(1)} %bitcast.45), channel_id=1, source_target_pairs={{0,10},{1,26},{2,12},{3,28},{4,14},{5,30},{6,8},{7,24},{8,2},{9,18... | collective-permute-start | bytes 393224 | tf_op jit(solution)/shard_map/ppermute | solution.py:59
  21.9 4.2 %collective-permute-start.7 = (bf16[256,256]{1,0:T(8,128)(2,1)S(1)}, bf16[256,256]{1,0:T(8,128)(2,1)S(1)}, u32[]{:S(2)}, u32[]{:S(2)}) collective-permute-start(bf16[256,256]{1,0:T(8,128)(2,1)S(1)} %bitcast.47), channel_id=1, source_target_pairs={{0,14},{1,30},{2,8},{3,24},{4,10},{5,26},{6,12},{7,28},{8,6},{9,22... | collective-permute-start | bytes 393224 | tf_op jit(solution)/shard_map/ppermute | solution.py:59
  27.6 4.1 %collective-permute-done.6.refs_6_ = bf16[256,256]{1,0:T(8,128)(2,1)S(1)} collective-permute-done((bf16[256,256]{1,0:T(8,128)(2,1)S(1)}, bf16[256,256]{1,0:T(8,128)(2,1)S(1)}, u32[]{:S(2)}, u32[]{:S(2)}) %collective-permute-start.6) | collective-permute-done | bytes 131104 | tf_op jit(solution)/shard_map/ppermute | solution.py:59
  31.6 2.5 collective-permute-done.7.refs_7_
  34.8 2.3 shard_map.110.own
  37.1 1.3 collective-permute-start.8
  39.9 1.2 broadcast_in_dim.26
  41.3 7.3 %all-to-all-start.2 = ((bf16[8,256,256]{2,1,0:T(8,128)(2,1)}), bf16[8,256,256]{2,1,0:T(8,128)(2,1)S(1)}, u32[]{:S(2)}, u32[]{:S(2)}) async-start(bf16[8,256,256]{2,1,0:T(8,128)(2,1)} %broadcast_in_dim.26), calls=%async_computation.2 | async-start | bytes 2097152 | tf_op jit(solution)/shard_map/all_to_all | solution.py:67
  48.6 1.0 copy-done.1
  49.6 3.3 %shard_map.111 = (f32[256,256]{1,0:T(8,128)}, bf16[256,256]{1,0:T(8,128)(2,1)}) custom-call(s32[4]{0:T(128)} %pad_add_fusion.at, bf16[8,256,256]{2,1,0:T(8,128)(2,1)} %copy-done.2, bf16[8,256,256]{2,1,0:T(8,128)(2,1)} %shard_map.110.own, bf16[8,256,256]{2,1,0:T(8,128)(2,1)} %copy-done.1), custom_call_target="tpu_custom_call" | custom-call | flops 536870912 | bytes 3538944 | tf_op jit(solution)/shard_map/pallas_call | solution.py:114
  52.9 4.3 %collective-permute-start.9 = (bf16[256,256]{1,0:T(8,128)(2,1)}, bf16[256,256]{1,0:T(8,128)(2,1)S(1)}, u32[]{:S(2)}, u32[]{:S(2)}) collective-permute-start(bf16[256,256]{1,0:T(8,128)(2,1)} %get-tuple-element.28), channel_id=1, source_target_pairs={{0,16},{16,0},{32,48},{48,32},{64,80},{80,64},{96,112},{112,96},{1... | collective-permute-start | bytes 393224 | tf_op jit(solution)/shard_map/ppermute | solution.py:40
  57.3 8.9 %collective-permute-done.9 = bf16[256,256]{1,0:T(8,128)(2,1)S(1)} collective-permute-done((bf16[256,256]{1,0:T(8,128)(2,1)}, bf16[256,256]{1,0:T(8,128)(2,1)S(1)}, u32[]{:S(2)}, u32[]{:S(2)}) %collective-permute-start.9) | collective-permute-done | bytes 131104 | tf_op jit(solution)/shard_map/ppermute | solution.py:40
  66.2 1.0 add_convert_fusion
  67.2 1.2 broadcast_in_dim.25
  68.4 5.6 %all-to-all-start.1 = ((bf16[8,256,256]{2,1,0:T(8,128)(2,1)}), bf16[8,256,256]{2,1,0:T(8,128)(2,1)}, u32[]{:S(2)}, u32[]{:S(2)}) async-start(bf16[8,256,256]{2,1,0:T(8,128)(2,1)} %broadcast_in_dim.25), calls=%async_computation.1 | async-start | bytes 2097152 | tf_op jit(solution)/shard_map/all_to_all | solution.py:67
  74.1 1.6 collective-permute-start.37
  75.7 2.5 collective-permute-start.38
  78.2 24.6 %all-to-all-done.1.blocks = bf16[8,256,256]{2,1,0:T(8,128)(2,1)} async-done(((bf16[8,256,256]{2,1,0:T(8,128)(2,1)}), bf16[8,256,256]{2,1,0:T(8,128)(2,1)}, u32[]{:S(2)}, u32[]{:S(2)}) %all-to-all-start.1) | async-done | bytes 1048608 | tf_op jit(solution)/shard_map/all_to_all | solution.py:67
  102.9 3.3 %shard_map.112 = (f32[256,256]{1,0:T(8,128)}, bf16[256,256]{1,0:T(8,128)(2,1)}) custom-call(s32[4]{0:T(128)} %pad_add_fusion.at, bf16[8,256,256]{2,1,0:T(8,128)(2,1)} %all-to-all-done.1.blocks, bf16[8,256,256]{2,1,0:T(8,128)(2,1)} %copy-done, bf16[8,256,256]{2,1,0:T(8,128)(2,1)} %copy-done.4), custom_call_target="tpu_custom_call" | custom-call | flops 536870912 | bytes 3538944 | tf_op jit(solution)/shard_map/pallas_call | solution.py:114
  106.2 1.1 collective-permute-start.12
  107.3 4.5 %collective-permute-done.12 = bf16[256,256]{1,0:T(8,128)(2,1)S(1)} collective-permute-done((bf16[256,256]{1,0:T(8,128)(2,1)}, bf16[256,256]{1,0:T(8,128)(2,1)S(1)}, u32[]{:S(2)}, u32[]{:S(2)}) %collective-permute-start.12) | collective-permute-done | bytes 131104 | tf_op jit(solution)/shard_map/ppermute | solution.py:40
  111.8 2.0 divide_convert_fusion
  113.8 1.3 collective-permute-done.39.beside
  115.8 3.8 %shard_map.116 = bf16[8,256,256]{2,1,0:T(8,128)(2,1)} custom-call(s32[4]{0:T(128)} %pad_add_fusion.at, bf16[8,256,256]{2,1,0:T(8,128)(2,1)} %collective-permute-done.37.first, bf16[8,256,256]{2,1,0:T(8,128)(2,1)} %collective-permute-done.38.second, bf16[256,256]{1,0:T(8,128)(2,1)} %copy-done.7, bf16[256,256]{1,0:T(8,128)(2,1)} %copy-done.23), custom_call_target="tpu_custom_call" | custom-call | flops 536870912 | bytes 3407872 | tf_op jit(solution)/shard_map/pallas_call | solution.py:114
  119.6 6.2 %all-to-all-start.3 = ((bf16[8,256,256]{2,1,0:T(8,128)(2,1)}), bf16[8,256,256]{2,1,0:T(8,128)(2,1)S(1)}, u32[]{:S(2)}, u32[]{:S(2)}) async-start(bf16[8,256,256]{2,1,0:T(8,128)(2,1)} %shard_map.116), calls=%async_computation.3 | async-start | bytes 2097152 | tf_op jit(solution)/shard_map/all_to_all | solution.py:67
  125.8 1.0 collective-permute-start.13
  126.9 3.1 %collective-permute-start.23 = (bf16[256,256]{1,0:T(8,128)(2,1)S(1)}, bf16[256,256]{1,0:T(8,128)(2,1)S(1)}, u32[]{:S(2)}, u32[]{:S(2)}) collective-permute-start(bf16[256,256]{1,0:T(8,128)(2,1)S(1)} %bitcast.51), channel_id=1, source_target_pairs={{0,96},{16,112},{32,128},{48,144},{64,160},{80,176},{96,192},{112,... | collective-permute-start | bytes 393224 | tf_op jit(solution)/shard_map/ppermute | solution.py:32
  130.0 3.3 %collective-permute-start.24 = (bf16[256,256]{1,0:T(8,128)(2,1)S(1)}, bf16[256,256]{1,0:T(8,128)(2,1)S(1)}, u32[]{:S(2)}, u32[]{:S(2)}) collective-permute-start(bf16[256,256]{1,0:T(8,128)(2,1)S(1)} %bitcast.52), channel_id=1, source_target_pairs={{0,128},{16,144},{32,160},{48,176},{64,192},{80,208},{96,224},{112... | collective-permute-start | bytes 393224 | tf_op jit(solution)/shard_map/ppermute | solution.py:32
  133.3 8.2 %collective-permute-done.13.beside.refs_9_ = bf16[256,256]{1,0:T(8,128)(2,1)S(1)} collective-permute-done((bf16[256,256]{1,0:T(8,128)(2,1)S(1)}, bf16[256,256]{1,0:T(8,128)(2,1)S(1)}, u32[]{:S(2)}, u32[]{:S(2)}) %collective-permute-start.13) | collective-permute-done | bytes 131104 | tf_op jit(solution)/shard_map/ppermute | solution.py:40
  141.6 1.5 collective-permute-start.26
  143.0 2.4 collective-permute-start.27
  145.6 2.6 %collective-permute-done.23.refs_3_ = bf16[256,256]{1,0:T(8,128)(2,1)S(1)} collective-permute-done((bf16[256,256]{1,0:T(8,128)(2,1)S(1)}, bf16[256,256]{1,0:T(8,128)(2,1)S(1)}, u32[]{:S(2)}, u32[]{:S(2)}) %collective-permute-start.23) | collective-permute-done | bytes 131104 | tf_op jit(solution)/shard_map/ppermute | solution.py:32
  148.3 1.0 collective-permute-start.40
  149.3 1.1 collective-permute-done.25.refs_5_
  150.4 4.0 %collective-permute-done.26.refs_6_ = bf16[256,256]{1,0:T(8,128)(2,1)S(1)} collective-permute-done((bf16[256,256]{1,0:T(8,128)(2,1)S(1)}, bf16[256,256]{1,0:T(8,128)(2,1)S(1)}, u32[]{:S(2)}, u32[]{:S(2)}) %collective-permute-start.26) | collective-permute-done | bytes 131104 | tf_op jit(solution)/shard_map/ppermute | solution.py:32
  154.3 2.0 collective-permute-done.27.refs_7_
  157.1 4.9 %shard_map.114 = (bf16[8,256,256]{2,1,0:T(8,128)(2,1)}, bf16[8,256,256]{2,1,0:T(8,128)(2,1)}) custom-call(s32[4]{0:T(128)} %pad_add_fusion.at, bf16[256,256]{1,0:T(8,128)(2,1)} %bitcast.37, bf16[256,256]{1,0:T(8,128)(2,1)} %copy-done.30, bf16[256,256]{1,0:T(8,128)(2,1)} %copy-done.31, bf16[256,256]{1,0:T(8,128)(2,1)} %copy-done.32, ...), custom_call_target="tpu_custom_call" | custom-call | flops 536870912 | bytes 3407872 | tf_op jit(solution)/shard_map/pallas_call | solution.py:114
  162.6 4.0 %shard_map.117 = bf16[8,256,256]{2,1,0:T(8,128)(2,1)} custom-call(s32[4]{0:T(128)} %pad_add_fusion.at, bf16[256,256]{1,0:T(8,128)(2,1)} %copy-done.6, bf16[256,256]{1,0:T(8,128)(2,1)} %copy-done.22, bf16[8,256,256]{2,1,0:T(8,128)(2,1)} %copy-done, bf16[8,256,256]{2,1,0:T(8,128)(2,1)} %copy-done.4), custom_call_target="tpu_custom_call" | custom-call | flops 536870912 | bytes 3407872 | tf_op jit(solution)/shard_map/pallas_call | solution.py:114
  166.7 5.8 %all-to-all-start.4 = ((bf16[8,256,256]{2,1,0:T(8,128)(2,1)}), bf16[8,256,256]{2,1,0:T(8,128)(2,1)S(1)}, u32[]{:S(2)}, u32[]{:S(2)}) async-start(bf16[8,256,256]{2,1,0:T(8,128)(2,1)} %shard_map.117), calls=%async_computation.4 | async-start | bytes 2097152 | tf_op jit(solution)/shard_map/all_to_all | solution.py:67
  172.4 4.2 %shard_map.113 = (f32[256,256]{1,0:T(8,128)}, bf16[256,256]{1,0:T(8,128)(2,1)}, bf16[256,256]{1,0:T(8,128)(2,1)}, bf16[256,256]{1,0:T(8,128)(2,1)}, bf16[256,256...) custom-call(s32[4]{0:T(128)} %pad_add_fusion.at, ...), custom_call_target="tpu_custom_call" | custom-call | flops 536870912 | bytes 3538944 | tf_op jit(solution)/shard_map/pallas_call | solution.py:114
  176.6 3.2 %collective-permute-start.20 = (bf16[256,256]{1,0:T(8,128)(2,1)}, bf16[256,256]{1,0:T(8,128)(2,1)S(1)}, u32[]{:S(2)}, u32[]{:S(2)}) collective-permute-start(bf16[256,256]{1,0:T(8,128)(2,1)} %get-tuple-element.38), channel_id=1, source_target_pairs={{0,224},{16,240},{32,0},{48,16},{64,32},{80,48},{96,64},{112,80},{... | collective-permute-start | bytes 393224 | tf_op jit(solution)/shard_map/ppermute | solution.py:32
  179.8 2.4 collective-permute-start.19
  183.2 2.8 %shard_map.115 = (bf16[256,256]{1,0:T(8,128)(2,1)}, bf16[256,256]{1,0:T(8,128)(2,1)}, bf16[256,256]{1,0:T(8,128)(2,1)}, bf16[256,256]{1,0:T(8,128)(2,1)}, bf16[2...) custom-call(s32[4]{0:T(128)} %pad_add_fusion.at, ...), custom_call_target="tpu_custom_call" | custom-call | bytes 3145728 | tf_op jit(solution)/shard_map/pallas_call | solution.py:114
  186.0 4.9 %collective-permute-start.36 = (bf16[256,256]{1,0:T(8,128)(2,1)}, bf16[256,256]{1,0:T(8,128)(2,1)S(1)}, u32[]{:S(2)}, u32[]{:S(2)}) collective-permute-start(bf16[256,256]{1,0:T(8,128)(2,1)} %get-tuple-element.48), channel_id=1, source_target_pairs={{0,14},{1,30},{2,8},{3,24},{4,10},{5,26},{6,12},{7,28},{8,6},{9,22... | collective-permute-start | bytes 393224 | tf_op jit(solution)/shard_map/ppermute | solution.py:59
  190.8 3.1 %collective-permute-start.35 = (bf16[256,256]{1,0:T(8,128)(2,1)}, bf16[256,256]{1,0:T(8,128)(2,1)S(1)}, u32[]{:S(2)}, u32[]{:S(2)}) collective-permute-start(bf16[256,256]{1,0:T(8,128)(2,1)} %get-tuple-element.47), channel_id=1, source_target_pairs={{0,12},{1,28},{2,14},{3,30},{4,8},{5,24},{6,10},{7,26},{8,4},{9,20... | collective-permute-start | bytes 393224 | tf_op jit(solution)/shard_map/ppermute | solution.py:59
  193.9 1.1 collective-permute-start.34
  195.0 7.1 %collective-permute-done.20 = bf16[256,256]{1,0:T(8,128)(2,1)S(1)} collective-permute-done((bf16[256,256]{1,0:T(8,128)(2,1)}, bf16[256,256]{1,0:T(8,128)(2,1)S(1)}, u32[]{:S(2)}, u32[]{:S(2)}) %collective-permute-start.20) | collective-permute-done | bytes 131104 | tf_op jit(solution)/shard_map/ppermute | solution.py:32
  202.2 5.0 %collective-permute-done.19 = bf16[256,256]{1,0:T(8,128)(2,1)S(1)} collective-permute-done((bf16[256,256]{1,0:T(8,128)(2,1)}, bf16[256,256]{1,0:T(8,128)(2,1)S(1)}, u32[]{:S(2)}, u32[]{:S(2)}) %collective-permute-start.19) | collective-permute-done | bytes 131104 | tf_op jit(solution)/shard_map/ppermute | solution.py:32
  207.2 5.8 %collective-permute-start.32 = (bf16[256,256]{1,0:T(8,128)(2,1)}, bf16[256,256]{1,0:T(8,128)(2,1)S(1)}, u32[]{:S(2)}, u32[]{:S(2)}) collective-permute-start(bf16[256,256]{1,0:T(8,128)(2,1)} %get-tuple-element.44), channel_id=1, source_target_pairs={{0,6},{1,22},{2,0},{3,16},{4,2},{5,18},{6,4},{7,20},{8,14},{9,30},... | collective-permute-start | bytes 393224 | tf_op jit(solution)/shard_map/ppermute | solution.py:59
  213.3 1.4 collective-permute-start.30
  214.7 1.6 collective-permute-start.29
  216.3 2.7 %collective-permute-start.18 = (bf16[256,256]{1,0:T(8,128)(2,1)S(1)}, bf16[256,256]{1,0:T(8,128)(2,1)S(1)}, u32[]{:S(2)}, u32[]{:S(2)}) collective-permute-start(bf16[256,256]{1,0:T(8,128)(2,1)S(1)} %copy-done.29), channel_id=1, source_target_pairs={{0,160},{16,176},{32,192},{48,208},{64,224},{80,240},{96,0},{112,1... | collective-permute-start | bytes 393224 | tf_op jit(solution)/shard_map/ppermute | solution.py:32
  219.9 3.4 %collective-permute-start.17 = (bf16[256,256]{1,0:T(8,128)(2,1)S(1)}, bf16[256,256]{1,0:T(8,128)(2,1)S(1)}, u32[]{:S(2)}, u32[]{:S(2)}) collective-permute-start(bf16[256,256]{1,0:T(8,128)(2,1)S(1)} %copy-done.28), channel_id=1, source_target_pairs={{0,128},{16,144},{32,160},{48,176},{64,192},{80,208},{96,224},{112... | collective-permute-start | bytes 393224 | tf_op jit(solution)/shard_map/ppermute | solution.py:32
  223.3 1.4 collective-permute-start.16
  224.7 1.2 collective-permute-start.15
  225.9 4.0 %collective-permute-start.14 = (bf16[256,256]{1,0:T(8,128)(2,1)S(1)}, bf16[256,256]{1,0:T(8,128)(2,1)S(1)}, u32[]{:S(2)}, u32[]{:S(2)}) collective-permute-start(bf16[256,256]{1,0:T(8,128)(2,1)S(1)} %copy-done.25), channel_id=1, source_target_pairs={{0,32},{16,48},{32,64},{48,80},{64,96},{80,112},{96,128},{112,144}... | collective-permute-start | bytes 393224 | tf_op jit(solution)/shard_map/ppermute | solution.py:32
  230.8 11.6 %collective-permute-done.16 = bf16[256,256]{1,0:T(8,128)(2,1)S(1)} collective-permute-done((bf16[256,256]{1,0:T(8,128)(2,1)S(1)}, bf16[256,256]{1,0:T(8,128)(2,1)S(1)}, u32[]{:S(2)}, u32[]{:S(2)}) %collective-permute-start.16) | collective-permute-done | bytes 131104 | tf_op jit(solution)/shard_map/ppermute | solution.py:32
  242.4 4.2 %collective-permute-done.15 = bf16[256,256]{1,0:T(8,128)(2,1)S(1)} collective-permute-done((bf16[256,256]{1,0:T(8,128)(2,1)S(1)}, bf16[256,256]{1,0:T(8,128)(2,1)S(1)}, u32[]{:S(2)}, u32[]{:S(2)}) %collective-permute-start.15) | collective-permute-done | bytes 131104 | tf_op jit(solution)/shard_map/ppermute | solution.py:32
  246.5 2.8 %collective-permute-done.14 = bf16[256,256]{1,0:T(8,128)(2,1)S(1)} collective-permute-done((bf16[256,256]{1,0:T(8,128)(2,1)S(1)}, bf16[256,256]{1,0:T(8,128)(2,1)S(1)}, u32[]{:S(2)}, u32[]{:S(2)}) %collective-permute-start.14) | collective-permute-done | bytes 131104 | tf_op jit(solution)/shard_map/ppermute | solution.py:32
  (120 shorter events, 12.9 us)
Async XLA Ops:
  2.6 8.6 %copy-start.12 = (bf16[1,256,256]{2,1,0:T(8,128)(2,1)S(1)}, bf16[1,256,256]{2,1,0:T(8,128)(2,1)}, u32[]{:S(2)}) copy-start(bf16[1,256,256]{2,1,0:T(8,128)(2,1)} %param.7) | copy-start | bytes 393220
  2.6 37.3 %all-to-all-start = ((bf16[8,256,256]{2,1,0:T(8,128)(2,1)}), bf16[8,256,256]{2,1,0:T(8,128)(2,1)S(1)}, u32[]{:S(2)}, u32[]{:S(2)}) async-start(bf16[8,256,256]{2,1,0:T(8,128)(2,1)} %broadcast_in_dim.24), calls=%async_computation | async-start | bytes 2097152 | tf_op jit(solution)/shard_map/all_to_all | solution.py:67
  11.2 6.7 %collective-permute-start = (bf16[256,256]{1,0:T(8,128)(2,1)S(1)}, bf16[256,256]{1,0:T(8,128)(2,1)S(1)}, u32[]{:S(2)}, u32[]{:S(2)}) collective-permute-start(bf16[256,256]{1,0:T(8,128)(2,1)S(1)} %bitcast.40), channel_id=1, source_target_pairs={{0,0},{1,16},{2,2},{3,18},{4,4},{5,20},{6,6},{7,22},{8,8},{9,24},{... | collective-permute-start | bytes 393224 | tf_op jit(solution)/shard_map/ppermute | solution.py:59
  11.9 9.3 %collective-permute-start.1 = (bf16[256,256]{1,0:T(8,128)(2,1)S(1)}, bf16[256,256]{1,0:T(8,128)(2,1)S(1)}, u32[]{:S(2)}, u32[]{:S(2)}) collective-permute-start(bf16[256,256]{1,0:T(8,128)(2,1)S(1)} %bitcast.41), channel_id=1, source_target_pairs={{0,2},{1,18},{2,4},{3,20},{4,6},{5,22},{6,0},{7,16},{8,10},{9,26},... | collective-permute-start | bytes 393224 | tf_op jit(solution)/shard_map/ppermute | solution.py:59
  13.4 8.5 %collective-permute-start.2 = (bf16[256,256]{1,0:T(8,128)(2,1)S(1)}, bf16[256,256]{1,0:T(8,128)(2,1)S(1)}, u32[]{:S(2)}, u32[]{:S(2)}) collective-permute-start(bf16[256,256]{1,0:T(8,128)(2,1)S(1)} %bitcast.42), channel_id=1, source_target_pairs={{0,4},{1,20},{2,6},{3,22},{4,0},{5,16},{6,2},{7,18},{8,12},{9,28},... | collective-permute-start | bytes 393224 | tf_op jit(solution)/shard_map/ppermute | solution.py:59
  16.2 10.6 %collective-permute-start.3 = (bf16[256,256]{1,0:T(8,128)(2,1)S(1)}, bf16[256,256]{1,0:T(8,128)(2,1)S(1)}, u32[]{:S(2)}, u32[]{:S(2)}) collective-permute-start(bf16[256,256]{1,0:T(8,128)(2,1)S(1)} %bitcast.43), channel_id=1, source_target_pairs={{0,6},{1,22},{2,0},{3,16},{4,2},{5,18},{6,4},{7,20},{8,14},{9,30},... | collective-permute-start | bytes 393224 | tf_op jit(solution)/shard_map/ppermute | solution.py:59
  17.6 10.0 %collective-permute-start.4 = (bf16[256,256]{1,0:T(8,128)(2,1)S(1)}, bf16[256,256]{1,0:T(8,128)(2,1)S(1)}, u32[]{:S(2)}, u32[]{:S(2)}) collective-permute-start(bf16[256,256]{1,0:T(8,128)(2,1)S(1)} %bitcast.44), channel_id=1, source_target_pairs={{0,8},{1,24},{2,10},{3,26},{4,12},{5,28},{6,14},{7,30},{8,0},{9,16... | collective-permute-start | bytes 393224 | tf_op jit(solution)/shard_map/ppermute | solution.py:59
  17.9 16.2 %copy-start.14 = (bf16[256,256]{1,0:T(8,128)(2,1)}, bf16[256,256]{1,0:T(8,128)(2,1)S(1)}, u32[]{:S(2)}) copy-start(bf16[256,256]{1,0:T(8,128)(2,1)S(1)} %collective-permute-done.refs_0_) | copy-start | bytes 393220
  18.0 9.6 %collective-permute-start.5 = (bf16[256,256]{1,0:T(8,128)(2,1)S(1)}, bf16[256,256]{1,0:T(8,128)(2,1)S(1)}, u32[]{:S(2)}, u32[]{:S(2)}) collective-permute-start(bf16[256,256]{1,0:T(8,128)(2,1)S(1)} %bitcast.45), channel_id=1, source_target_pairs={{0,10},{1,26},{2,12},{3,28},{4,14},{5,30},{6,8},{7,24},{8,2},{9,18... | collective-permute-start | bytes 393224 | tf_op jit(solution)/shard_map/ppermute | solution.py:59
  21.2 12.9 %copy-start.15 = (bf16[256,256]{1,0:T(8,128)(2,1)}, bf16[256,256]{1,0:T(8,128)(2,1)S(1)}, u32[]{:S(2)}) copy-start(bf16[256,256]{1,0:T(8,128)(2,1)S(1)} %collective-permute-done.1.refs_1_) | copy-start | bytes 393220
  21.2 10.4 %collective-permute-start.6 = (bf16[256,256]{1,0:T(8,128)(2,1)S(1)}, bf16[256,256]{1,0:T(8,128)(2,1)S(1)}, u32[]{:S(2)}, u32[]{:S(2)}) collective-permute-start(bf16[256,256]{1,0:T(8,128)(2,1)S(1)} %bitcast.46), channel_id=1, source_target_pairs={{0,12},{1,28},{2,14},{3,30},{4,8},{5,24},{6,10},{7,26},{8,4},{9,20... | collective-permute-start | bytes 393224 | tf_op jit(solution)/shard_map/ppermute | solution.py:59
  21.9 12.2 %copy-start.16 = (bf16[256,256]{1,0:T(8,128)(2,1)}, bf16[256,256]{1,0:T(8,128)(2,1)S(1)}, u32[]{:S(2)}) copy-start(bf16[256,256]{1,0:T(8,128)(2,1)S(1)} %collective-permute-done.2.refs_2_) | copy-start | bytes 393220
  21.9 12.2 %collective-permute-start.7 = (bf16[256,256]{1,0:T(8,128)(2,1)S(1)}, bf16[256,256]{1,0:T(8,128)(2,1)S(1)}, u32[]{:S(2)}, u32[]{:S(2)}) collective-permute-start(bf16[256,256]{1,0:T(8,128)(2,1)S(1)} %bitcast.47), channel_id=1, source_target_pairs={{0,14},{1,30},{2,8},{3,24},{4,10},{5,26},{6,12},{7,28},{8,6},{9,22... | collective-permute-start | bytes 393224 | tf_op jit(solution)/shard_map/ppermute | solution.py:59
  26.8 11.7 %copy-start.24 = (bf16[1,256,256]{2,1,0:T(8,128)(2,1)S(1)}, bf16[1,256,256]{2,1,0:T(8,128)(2,1)}, u32[]{:S(2)}) copy-start(bf16[1,256,256]{2,1,0:T(8,128)(2,1)} %param.13) | copy-start | bytes 393220
  26.8 7.4 %copy-start.17 = (bf16[256,256]{1,0:T(8,128)(2,1)}, bf16[256,256]{1,0:T(8,128)(2,1)S(1)}, u32[]{:S(2)}) copy-start(bf16[256,256]{1,0:T(8,128)(2,1)S(1)} %collective-permute-done.3.refs_3_) | copy-start | bytes 393220
  37.1 11.4 %collective-permute-start.8 = (bf16[8,256,256]{2,1,0:T(8,128)(2,1)}, bf16[8,256,256]{2,1,0:T(8,128)(2,1)S(1)}, u32[]{:S(2)}, u32[]{:S(2)}) collective-permute-start(bf16[8,256,256]{2,1,0:T(8,128)(2,1)} %shard_map.110.own), channel_id=1, source_target_pairs={{0,1},{1,0},{2,3},{3,2},{4,5},{5,4},{6,7},{7,6},{8,9},{9,8},{10,11... | collective-permute-start | bytes 3145736 | tf_op jit(solution)/shard_map/ppermute | solution.py:36
  38.5 0.7 collective-permute-start.10
  41.3 25.8 %all-to-all-start.2 = ((bf16[8,256,256]{2,1,0:T(8,128)(2,1)}), bf16[8,256,256]{2,1,0:T(8,128)(2,1)S(1)}, u32[]{:S(2)}, u32[]{:S(2)}) async-start(bf16[8,256,256]{2,1,0:T(8,128)(2,1)} %broadcast_in_dim.26), calls=%async_computation.2 | async-start | bytes 2097152 | tf_op jit(solution)/shard_map/all_to_all | solution.py:67
  52.9 13.3 %collective-permute-start.9 = (bf16[256,256]{1,0:T(8,128)(2,1)}, bf16[256,256]{1,0:T(8,128)(2,1)S(1)}, u32[]{:S(2)}, u32[]{:S(2)}) collective-permute-start(bf16[256,256]{1,0:T(8,128)(2,1)} %get-tuple-element.28), channel_id=1, source_target_pairs={{0,16},{16,0},{32,48},{48,32},{64,80},{80,64},{96,112},{112,96},{1... | collective-permute-start | bytes 393224 | tf_op jit(solution)/shard_map/ppermute | solution.py:40
  68.4 34.5 %all-to-all-start.1 = ((bf16[8,256,256]{2,1,0:T(8,128)(2,1)}), bf16[8,256,256]{2,1,0:T(8,128)(2,1)}, u32[]{:S(2)}, u32[]{:S(2)}) async-start(bf16[8,256,256]{2,1,0:T(8,128)(2,1)} %broadcast_in_dim.25), calls=%async_computation.1 | async-start | bytes 2097152 | tf_op jit(solution)/shard_map/all_to_all | solution.py:67
  74.0 37.8 %copy-start.8 = (f32[1,256,256]{2,1,0:T(8,128)S(1)}, f32[1,256,256]{2,1,0:T(8,128)}, u32[]{:S(2)}) copy-start(f32[1,256,256]{2,1,0:T(8,128)} %param.8) | copy-start | bytes 786436
  74.0 4.2 %collective-permute-start.11 = (bf16[8,256,256]{2,1,0:T(8,128)(2,1)S(1)}, bf16[8,256,256]{2,1,0:T(8,128)(2,1)S(1)}, u32[]{:S(2)}, u32[]{:S(2)}) collective-permute-start(bf16[8,256,256]{2,1,0:T(8,128)(2,1)S(1)} %all-to-all-done.2.own), channel_id=1, source_target_pairs={{0,1},{1,0},{2,3},{3,2},{4,5},{5,4},{6,7},{7,6},{8,9},{9,8},{10,11... | collective-permute-start | bytes 3145736 | tf_op jit(solution)/shard_map/ppermute | solution.py:36
  74.1 39.7 %collective-permute-start.37 = (bf16[8,256,256]{2,1,0:T(8,128)(2,1)S(1)}, bf16[8,256,256]{2,1,0:T(8,128)(2,1)}, u32[]{:S(2)}, u32[]{:S(2)}) collective-permute-start(bf16[8,256,256]{2,1,0:T(8,128)(2,1)S(1)} %copy-done.3), channel_id=1, source_target_pairs={{0,0},{16,1},{2,2},{18,3},{4,4},{20,5},{6,6},{22,7},{8,8},{24,9},{... | collective-permute-start | bytes 3145736 | tf_op jit(solution)/shard_map/ppermute | solution.py:49
  75.7 38.1 %collective-permute-start.38 = (bf16[8,256,256]{2,1,0:T(8,128)(2,1)S(1)}, bf16[8,256,256]{2,1,0:T(8,128)(2,1)}, u32[]{:S(2)}, u32[]{:S(2)}) collective-permute-start(bf16[8,256,256]{2,1,0:T(8,128)(2,1)S(1)} %copy-done.3), channel_id=1, source_target_pairs={{1,0},{17,1},{3,2},{19,3},{5,4},{21,5},{7,6},{23,7},{9,8},{25,9},{... | collective-permute-start | bytes 3145736 | tf_op jit(solution)/shard_map/ppermute | solution.py:49
  78.2 24.6 %copy-start.4 = (bf16[8,256,256]{2,1,0:T(8,128)(2,1)}, bf16[8,256,256]{2,1,0:T(8,128)(2,1)S(1)}, u32[]{:S(2)}) copy-start(bf16[8,256,256]{2,1,0:T(8,128)(2,1)S(1)} %collective-permute-done.11.other) | copy-start | bytes 3145732
  106.2 5.6 %collective-permute-start.12 = (bf16[256,256]{1,0:T(8,128)(2,1)}, bf16[256,256]{1,0:T(8,128)(2,1)S(1)}, u32[]{:S(2)}, u32[]{:S(2)}) collective-permute-start(bf16[256,256]{1,0:T(8,128)(2,1)} %get-tuple-element.30), channel_id=1, source_target_pairs={{0,16},{16,0},{32,48},{48,32},{64,80},{80,64},{96,112},{112,96},{1... | collective-permute-start | bytes 393224 | tf_op jit(solution)/shard_map/ppermute | solution.py:40
  113.8 1.3 collective-permute-start.39
  119.6 25.9 %all-to-all-start.3 = ((bf16[8,256,256]{2,1,0:T(8,128)(2,1)}), bf16[8,256,256]{2,1,0:T(8,128)(2,1)S(1)}, u32[]{:S(2)}, u32[]{:S(2)}) async-start(bf16[8,256,256]{2,1,0:T(8,128)(2,1)} %shard_map.116), calls=%async_computation.3 | async-start | bytes 2097152 | tf_op jit(solution)/shard_map/all_to_all | solution.py:67
  125.8 15.7 %collective-permute-start.13 = (bf16[256,256]{1,0:T(8,128)(2,1)S(1)}, bf16[256,256]{1,0:T(8,128)(2,1)S(1)}, u32[]{:S(2)}, u32[]{:S(2)}) collective-permute-start(bf16[256,256]{1,0:T(8,128)(2,1)S(1)} %bitcast.48), channel_id=1, source_target_pairs={{0,16},{16,0},{32,48},{48,32},{64,80},{80,64},{96,112},{112,96},{1... | collective-permute-start | bytes 393224 | tf_op jit(solution)/shard_map/ppermute | solution.py:40
  126.8 14.8 %collective-permute-start.21 = (bf16[256,256]{1,0:T(8,128)(2,1)S(1)}, bf16[256,256]{1,0:T(8,128)(2,1)S(1)}, u32[]{:S(2)}, u32[]{:S(2)}) collective-permute-start(bf16[256,256]{1,0:T(8,128)(2,1)S(1)} %bitcast.49), channel_id=1, source_target_pairs={{0,32},{16,48},{32,64},{48,80},{64,96},{80,112},{96,128},{112,144}... | collective-permute-start | bytes 393224 | tf_op jit(solution)/shard_map/ppermute | solution.py:32
  126.9 16.2 %collective-permute-start.22 = (bf16[256,256]{1,0:T(8,128)(2,1)S(1)}, bf16[256,256]{1,0:T(8,128)(2,1)S(1)}, u32[]{:S(2)}, u32[]{:S(2)}) collective-permute-start(bf16[256,256]{1,0:T(8,128)(2,1)S(1)} %bitcast.50), channel_id=1, source_target_pairs={{0,64},{16,80},{32,96},{48,112},{64,128},{80,144},{96,160},{112,17... | collective-permute-start | bytes 393224 | tf_op jit(solution)/shard_map/ppermute | solution.py:32
  126.9 21.4 %collective-permute-start.23 = (bf16[256,256]{1,0:T(8,128)(2,1)S(1)}, bf16[256,256]{1,0:T(8,128)(2,1)S(1)}, u32[]{:S(2)}, u32[]{:S(2)}) collective-permute-start(bf16[256,256]{1,0:T(8,128)(2,1)S(1)} %bitcast.51), channel_id=1, source_target_pairs={{0,96},{16,112},{32,128},{48,144},{64,160},{80,176},{96,192},{112,... | collective-permute-start | bytes 393224 | tf_op jit(solution)/shard_map/ppermute | solution.py:32
  130.0 19.3 %collective-permute-start.24 = (bf16[256,256]{1,0:T(8,128)(2,1)S(1)}, bf16[256,256]{1,0:T(8,128)(2,1)S(1)}, u32[]{:S(2)}, u32[]{:S(2)}) collective-permute-start(bf16[256,256]{1,0:T(8,128)(2,1)S(1)} %bitcast.52), channel_id=1, source_target_pairs={{0,128},{16,144},{32,160},{48,176},{64,192},{80,208},{96,224},{112... | collective-permute-start | bytes 393224 | tf_op jit(solution)/shard_map/ppermute | solution.py:32
  141.5 8.9 %collective-permute-start.25 = (bf16[256,256]{1,0:T(8,128)(2,1)S(1)}, bf16[256,256]{1,0:T(8,128)(2,1)S(1)}, u32[]{:S(2)}, u32[]{:S(2)}) collective-permute-start(bf16[256,256]{1,0:T(8,128)(2,1)S(1)} %bitcast.53), channel_id=1, source_target_pairs={{0,160},{16,176},{32,192},{48,208},{64,224},{80,240},{96,0},{112,1... | collective-permute-start | bytes 393224 | tf_op jit(solution)/shard_map/ppermute | solution.py:32
  141.6 12.8 %collective-permute-start.26 = (bf16[256,256]{1,0:T(8,128)(2,1)S(1)}, bf16[256,256]{1,0:T(8,128)(2,1)S(1)}, u32[]{:S(2)}, u32[]{:S(2)}) collective-permute-start(bf16[256,256]{1,0:T(8,128)(2,1)S(1)} %bitcast.54), channel_id=1, source_target_pairs={{0,192},{16,208},{32,224},{48,240},{64,0},{80,16},{96,32},{112,48}... | collective-permute-start | bytes 393224 | tf_op jit(solution)/shard_map/ppermute | solution.py:32
  143.0 13.3 %collective-permute-start.27 = (bf16[256,256]{1,0:T(8,128)(2,1)S(1)}, bf16[256,256]{1,0:T(8,128)(2,1)S(1)}, u32[]{:S(2)}, u32[]{:S(2)}) collective-permute-start(bf16[256,256]{1,0:T(8,128)(2,1)S(1)} %bitcast.55), channel_id=1, source_target_pairs={{0,224},{16,240},{32,0},{48,16},{64,32},{80,48},{96,64},{112,80},{... | collective-permute-start | bytes 393224 | tf_op jit(solution)/shard_map/ppermute | solution.py:32
  145.6 16.3 %copy-start.6 = (bf16[256,256]{1,0:T(8,128)(2,1)}, bf16[256,256]{1,0:T(8,128)(2,1)S(1)}, u32[]{:S(2)}) copy-start(bf16[256,256]{1,0:T(8,128)(2,1)S(1)} %reduce_sum.24.mine) | copy-start | bytes 393220
  148.3 8.1 %copy-start.32 = (bf16[256,256]{1,0:T(8,128)(2,1)}, bf16[256,256]{1,0:T(8,128)(2,1)S(1)}, u32[]{:S(2)}) copy-start(bf16[256,256]{1,0:T(8,128)(2,1)S(1)} %collective-permute-done.23.refs_3_) | copy-start | bytes 393220
  148.3 13.7 %collective-permute-start.40 = (bf16[256,256]{1,0:T(8,128)(2,1)S(1)}, bf16[256,256]{1,0:T(8,128)(2,1)S(1)}, u32[]{:S(2)}, u32[]{:S(2)}) collective-permute-start(bf16[256,256]{1,0:T(8,128)(2,1)S(1)} %reduce_sum.24.mine), channel_id=1, source_target_pairs={{0,16},{16,0},{32,48},{48,32},{64,80},{80,64},{96,112},{112,96},{1... | collective-permute-start | bytes 393224 | tf_op jit(solution)/shard_map/ppermute | solution.py:40
  161.9 20.3 %collective-permute-start.28 = (bf16[8,256,256]{2,1,0:T(8,128)(2,1)}, bf16[8,256,256]{2,1,0:T(8,128)(2,1)S(1)}, u32[]{:S(2)}, u32[]{:S(2)}) collective-permute-start(bf16[8,256,256]{2,1,0:T(8,128)(2,1)} %get-tuple-element.40), channel_id=1, source_target_pairs={{0,1},{1,0},{2,3},{3,2},{4,5},{5,4},{6,7},{7,6},{8,9},{9,8},{10,11... | collective-permute-start | bytes 3145736 | tf_op jit(solution)/shard_map/ppermute | solution.py:36
  166.7 83.5 %all-to-all-start.4 = ((bf16[8,256,256]{2,1,0:T(8,128)(2,1)}), bf16[8,256,256]{2,1,0:T(8,128)(2,1)S(1)}, u32[]{:S(2)}, u32[]{:S(2)}) async-start(bf16[8,256,256]{2,1,0:T(8,128)(2,1)} %shard_map.117), calls=%async_computation.4 | async-start | bytes 2097152 | tf_op jit(solution)/shard_map/all_to_all | solution.py:67
  176.6 25.5 %collective-permute-start.20 = (bf16[256,256]{1,0:T(8,128)(2,1)}, bf16[256,256]{1,0:T(8,128)(2,1)S(1)}, u32[]{:S(2)}, u32[]{:S(2)}) collective-permute-start(bf16[256,256]{1,0:T(8,128)(2,1)} %get-tuple-element.38), channel_id=1, source_target_pairs={{0,224},{16,240},{32,0},{48,16},{64,32},{80,48},{96,64},{112,80},{... | collective-permute-start | bytes 393224 | tf_op jit(solution)/shard_map/ppermute | solution.py:32
  179.8 27.4 %collective-permute-start.19 = (bf16[256,256]{1,0:T(8,128)(2,1)}, bf16[256,256]{1,0:T(8,128)(2,1)S(1)}, u32[]{:S(2)}, u32[]{:S(2)}) collective-permute-start(bf16[256,256]{1,0:T(8,128)(2,1)} %get-tuple-element.37), channel_id=1, source_target_pairs={{0,192},{16,208},{32,224},{48,240},{64,0},{80,16},{96,32},{112,48}... | collective-permute-start | bytes 393224 | tf_op jit(solution)/shard_map/ppermute | solution.py:32
  183.2 33.1 %copy-start.29 = (bf16[256,256]{1,0:T(8,128)(2,1)S(1)}, bf16[256,256]{1,0:T(8,128)(2,1)}, u32[]{:S(2)}) copy-start(bf16[256,256]{1,0:T(8,128)(2,1)} %get-tuple-element.36) | copy-start | bytes 393220
  183.2 36.7 %copy-start.28 = (bf16[256,256]{1,0:T(8,128)(2,1)S(1)}, bf16[256,256]{1,0:T(8,128)(2,1)}, u32[]{:S(2)}) copy-start(bf16[256,256]{1,0:T(8,128)(2,1)} %get-tuple-element.35) | copy-start | bytes 393220
  183.2 40.1 %copy-start.27 = (bf16[256,256]{1,0:T(8,128)(2,1)S(1)}, bf16[256,256]{1,0:T(8,128)(2,1)}, u32[]{:S(2)}) copy-start(bf16[256,256]{1,0:T(8,128)(2,1)} %get-tuple-element.34) | copy-start | bytes 393220
  183.2 41.5 %copy-start.26 = (bf16[256,256]{1,0:T(8,128)(2,1)S(1)}, bf16[256,256]{1,0:T(8,128)(2,1)}, u32[]{:S(2)}) copy-start(bf16[256,256]{1,0:T(8,128)(2,1)} %get-tuple-element.33) | copy-start | bytes 393220
  183.2 42.7 %copy-start.25 = (bf16[256,256]{1,0:T(8,128)(2,1)S(1)}, bf16[256,256]{1,0:T(8,128)(2,1)}, u32[]{:S(2)}) copy-start(bf16[256,256]{1,0:T(8,128)(2,1)} %get-tuple-element.32) | copy-start | bytes 393220
  183.2 46.7 %copy-start.9 = (f32[1,256,256]{2,1,0:T(8,128)S(1)}, f32[1,256,256]{2,1,0:T(8,128)}, u32[]{:S(2)}) copy-start(f32[1,256,256]{2,1,0:T(8,128)} %param.11) | copy-start | bytes 786436
  186.0 27.0 %collective-permute-start.36 = (bf16[256,256]{1,0:T(8,128)(2,1)}, bf16[256,256]{1,0:T(8,128)(2,1)S(1)}, u32[]{:S(2)}, u32[]{:S(2)}) collective-permute-start(bf16[256,256]{1,0:T(8,128)(2,1)} %get-tuple-element.48), channel_id=1, source_target_pairs={{0,14},{1,30},{2,8},{3,24},{4,10},{5,26},{6,12},{7,28},{8,6},{9,22... | collective-permute-start | bytes 393224 | tf_op jit(solution)/shard_map/ppermute | solution.py:59
  190.8 22.5 %collective-permute-start.35 = (bf16[256,256]{1,0:T(8,128)(2,1)}, bf16[256,256]{1,0:T(8,128)(2,1)S(1)}, u32[]{:S(2)}, u32[]{:S(2)}) collective-permute-start(bf16[256,256]{1,0:T(8,128)(2,1)} %get-tuple-element.47), channel_id=1, source_target_pairs={{0,12},{1,28},{2,14},{3,30},{4,8},{5,24},{6,10},{7,26},{8,4},{9,20... | collective-permute-start | bytes 393224 | tf_op jit(solution)/shard_map/ppermute | solution.py:59
  193.9 20.8 %collective-permute-start.34 = (bf16[256,256]{1,0:T(8,128)(2,1)}, bf16[256,256]{1,0:T(8,128)(2,1)S(1)}, u32[]{:S(2)}, u32[]{:S(2)}) collective-permute-start(bf16[256,256]{1,0:T(8,128)(2,1)} %get-tuple-element.46), channel_id=1, source_target_pairs={{0,10},{1,26},{2,12},{3,28},{4,14},{5,30},{6,8},{7,24},{8,2},{9,18... | collective-permute-start | bytes 393224 | tf_op jit(solution)/shard_map/ppermute | solution.py:59
  202.1 14.2 %collective-permute-start.33 = (bf16[256,256]{1,0:T(8,128)(2,1)}, bf16[256,256]{1,0:T(8,128)(2,1)S(1)}, u32[]{:S(2)}, u32[]{:S(2)}) collective-permute-start(bf16[256,256]{1,0:T(8,128)(2,1)} %get-tuple-element.45), channel_id=1, source_target_pairs={{0,8},{1,24},{2,10},{3,26},{4,12},{5,28},{6,14},{7,30},{8,0},{9,16... | collective-permute-start | bytes 393224 | tf_op jit(solution)/shard_map/ppermute | solution.py:59
  207.2 12.6 %collective-permute-start.32 = (bf16[256,256]{1,0:T(8,128)(2,1)}, bf16[256,256]{1,0:T(8,128)(2,1)S(1)}, u32[]{:S(2)}, u32[]{:S(2)}) collective-permute-start(bf16[256,256]{1,0:T(8,128)(2,1)} %get-tuple-element.44), channel_id=1, source_target_pairs={{0,6},{1,22},{2,0},{3,16},{4,2},{5,18},{6,4},{7,20},{8,14},{9,30},... | collective-permute-start | bytes 393224 | tf_op jit(solution)/shard_map/ppermute | solution.py:59
  213.0 10.3 %collective-permute-start.31 = (bf16[256,256]{1,0:T(8,128)(2,1)}, bf16[256,256]{1,0:T(8,128)(2,1)S(1)}, u32[]{:S(2)}, u32[]{:S(2)}) collective-permute-start(bf16[256,256]{1,0:T(8,128)(2,1)} %get-tuple-element.43), channel_id=1, source_target_pairs={{0,4},{1,20},{2,6},{3,22},{4,0},{5,16},{6,2},{7,18},{8,12},{9,28},... | collective-permute-start | bytes 393224 | tf_op jit(solution)/shard_map/ppermute | solution.py:59
  213.3 11.4 %collective-permute-start.30 = (bf16[256,256]{1,0:T(8,128)(2,1)}, bf16[256,256]{1,0:T(8,128)(2,1)S(1)}, u32[]{:S(2)}, u32[]{:S(2)}) collective-permute-start(bf16[256,256]{1,0:T(8,128)(2,1)} %get-tuple-element.42), channel_id=1, source_target_pairs={{0,2},{1,18},{2,4},{3,20},{4,6},{5,22},{6,0},{7,16},{8,10},{9,26},... | collective-permute-start | bytes 393224 | tf_op jit(solution)/shard_map/ppermute | solution.py:59
  214.7 11.2 %collective-permute-start.29 = (bf16[256,256]{1,0:T(8,128)(2,1)}, bf16[256,256]{1,0:T(8,128)(2,1)S(1)}, u32[]{:S(2)}, u32[]{:S(2)}) collective-permute-start(bf16[256,256]{1,0:T(8,128)(2,1)} %get-tuple-element.41), channel_id=1, source_target_pairs={{0,0},{1,16},{2,2},{3,18},{4,4},{5,20},{6,6},{7,22},{8,8},{9,24},{... | collective-permute-start | bytes 393224 | tf_op jit(solution)/shard_map/ppermute | solution.py:59
  216.3 14.5 %collective-permute-start.18 = (bf16[256,256]{1,0:T(8,128)(2,1)S(1)}, bf16[256,256]{1,0:T(8,128)(2,1)S(1)}, u32[]{:S(2)}, u32[]{:S(2)}) collective-permute-start(bf16[256,256]{1,0:T(8,128)(2,1)S(1)} %copy-done.29), channel_id=1, source_target_pairs={{0,160},{16,176},{32,192},{48,208},{64,224},{80,240},{96,0},{112,1... | collective-permute-start | bytes 393224 | tf_op jit(solution)/shard_map/ppermute | solution.py:32
  219.9 10.9 %collective-permute-start.17 = (bf16[256,256]{1,0:T(8,128)(2,1)S(1)}, bf16[256,256]{1,0:T(8,128)(2,1)S(1)}, u32[]{:S(2)}, u32[]{:S(2)}) collective-permute-start(bf16[256,256]{1,0:T(8,128)(2,1)S(1)} %copy-done.28), channel_id=1, source_target_pairs={{0,128},{16,144},{32,160},{48,176},{64,192},{80,208},{96,224},{112... | collective-permute-start | bytes 393224 | tf_op jit(solution)/shard_map/ppermute | solution.py:32
  223.3 19.1 %collective-permute-start.16 = (bf16[256,256]{1,0:T(8,128)(2,1)S(1)}, bf16[256,256]{1,0:T(8,128)(2,1)S(1)}, u32[]{:S(2)}, u32[]{:S(2)}) collective-permute-start(bf16[256,256]{1,0:T(8,128)(2,1)S(1)} %copy-done.27), channel_id=1, source_target_pairs={{0,96},{16,112},{32,128},{48,144},{64,160},{80,176},{96,192},{112,... | collective-permute-start | bytes 393224 | tf_op jit(solution)/shard_map/ppermute | solution.py:32
  224.7 21.9 %collective-permute-start.15 = (bf16[256,256]{1,0:T(8,128)(2,1)S(1)}, bf16[256,256]{1,0:T(8,128)(2,1)S(1)}, u32[]{:S(2)}, u32[]{:S(2)}) collective-permute-start(bf16[256,256]{1,0:T(8,128)(2,1)S(1)} %copy-done.26), channel_id=1, source_target_pairs={{0,64},{16,80},{32,96},{48,112},{64,128},{80,144},{96,160},{112,17... | collective-permute-start | bytes 393224 | tf_op jit(solution)/shard_map/ppermute | solution.py:32
  225.9 23.4 %copy-start.10 = (f32[1,256,256]{2,1,0:T(8,128)S(1)}, f32[1,256,256]{2,1,0:T(8,128)}, u32[]{:S(2)}) copy-start(f32[1,256,256]{2,1,0:T(8,128)} %param.10) | copy-start | bytes 786436
  225.9 23.4 %copy-start.11 = (f32[256,256]{1,0:T(8,128)S(1)}, f32[256,256]{1,0:T(8,128)}, u32[]{:S(2)}) copy-start(f32[256,256]{1,0:T(8,128)} %get-tuple-element.31) | copy-start | bytes 786436
  225.9 23.4 %collective-permute-start.14 = (bf16[256,256]{1,0:T(8,128)(2,1)S(1)}, bf16[256,256]{1,0:T(8,128)(2,1)S(1)}, u32[]{:S(2)}, u32[]{:S(2)}) collective-permute-start(bf16[256,256]{1,0:T(8,128)(2,1)S(1)} %copy-done.25), channel_id=1, source_target_pairs={{0,32},{16,48},{32,64},{48,80},{64,96},{80,112},{96,128},{112,144}... | collective-permute-start | bytes 393224 | tf_op jit(solution)/shard_map/ppermute | solution.py:32
  (19 other events, 61.4 us)
where the time goes:
time: 252 us; the launch traced here: 251 us
  starting transfers between devices  109 us (43%)
  waiting for transfers between devices  97.1 us (39%)
  Pallas kernels  28.6 us (11%)
  local copies, waits for them, and re-layouts  9.23 us (4%)
  other arithmetic  6.25 us (2%)
    ppermute x14, waiting for transfers between devices, along_z(): return lax.ppermute(x, 'dp', [(d, (d + 2 * s) % 16) for d in range(16)])  40.4 us
    ppermute x17, starting transfers between devices, to_swapped(): return lax.ppermute(x, ('dp', 'mp'), pairs)  33.7 us
    all_to_all x5, starting transfers between devices, exchange(): return lax.all_to_all(x, axis, 0, 0, axis_index_groups=groups, tiled=True)  33.4 us
    ppermute x14, starting transfers between devices, along_z(): return lax.ppermute(x, 'dp', [(d, (d + 2 * s) % 16) for d in range(16)])  28.7 us
    pallas_call x8, Pallas kernels, call(): pl.pallas_call(body, out_shape=outs, in_specs=[pl.BlockSpec(memory_space=...  28.6 us
    all_to_all x5, waiting for transfers between devices, exchange(): return lax.all_to_all(x, axis, 0, 0, axis_index_groups=groups, tiled=True)  25.4 us
    ppermute x4, waiting for transfers between devices, neighbour(): return lax.ppermute(x, 'dp', [(d, d ^ 1) for d in range(16)])  21.6 us
    ppermute x17, waiting for transfers between devices, to_swapped(): return lax.ppermute(x, ('dp', 'mp'), pairs)  8.39 us
  transfers between devices with their start and end apart: 46, of which 20 were waited for; matrix products, arithmetic and copies ran while one was open for 3% of the time, Pallas kernels for 10%

commit v1 on v0

v1 whole, which is shorter than its diff:
```python
import jax
import jax.numpy as jnp
from jax import lax
from jax.experimental import pallas as pl
from jax.experimental.pallas import tpu as pltpu
from jax.sharding import PartitionSpec as P


decay_moment = 0.95
decay_factor = 0.95
epsilon = 1e-08


N = 8
SIDE = 256
bf16, f32 = jnp.bfloat16, jnp.float32

TN = (((0,), (0,)), ((), ()))
NN = (((1,), (0,)), ((), ()))
NT = (((1,), (1,)), ((), ()))


def around(i, t):
    return (((i >> 2) + (t >> 2)) & 1) * 4 + ((i + t) & 3)


def back(i, t):
    return (((i >> 2) - (t >> 2)) & 1) * 4 + ((i - t) & 3)


def other_core(x):
    return lax.ppermute(x, "mp", [(m, m ^ 1) for m in range(16)])


def neighbour(x):
    return lax.ppermute(x, "dp", [(d, d ^ 1) for d in range(16)])


def placed(x, to):
    pairs = []
    for d in range(16):
        for m in range(16):
            to_d, to_m = to(d, m)
            pairs.append((d * 16 + m, to_d * 16 + to_m))
    return lax.ppermute(x, ("dp", "mp"), pairs)


def swap(d, m):
    return (d & ~1) | (m & 1), (m & ~1) | (d & 1)


def to_swapped(x, t):
    return placed(x, lambda d, m: swap(d, 2 * around(m >> 1, t) + (m & 1)))


Z_GROUPS = [[2 * z + y for z in range(N)] for y in range(2)]
PLANE_GROUPS = [[2 * i + c for i in range(N)] for c in range(2)]


def exchange(x, axis, groups):
    return lax.all_to_all(x, axis, 0, 0, axis_index_groups=groups, tiled=True)


def exchange_z(x):
    return exchange(x, "dp", Z_GROUPS)


def exchange_plane(x):
    return exchange(x, "mp", PLANE_GROUPS)


def everywhere_z(x):
    return exchange_z(jnp.broadcast_to(x, (N, *x.shape)))


def from_plane(x):
    arrived = {t: to_swapped(x, t) for t in (6, 5, 7, 2, 4, 1, 3, 0)}
    return [arrived[t] for t in range(N)]


def dot(a, b, dims):
    return lax.dot_general(a, b, dims, preferred_element_type=f32)


def plane_back(at, t):
    return back(at[1], t)


def plane_on(at, t):
    return around(at[1], t)


BLOCK = jax.ShapeDtypeStruct((SIDE, SIDE), bf16)
WIDE = jax.ShapeDtypeStruct((SIDE, SIDE), f32)
PANEL = jax.ShapeDtypeStruct((N, SIDE, SIDE), bf16)


def call(body, at, operands, outs, scratch=(), products=0, part=None):
    vmem = pl.BlockSpec(memory_space=pltpu.VMEM)
    first = vmem
    if part is not None:
        first = pl.BlockSpec((None, N, SIDE, SIDE), lambda _: (part, 0, 0, 0))
    moved = sum(o.size * o.dtype.itemsize for o in (*operands, *outs))
    return pl.pallas_call(
        body,
        out_shape=outs,
        grid=() if part is None else (1,),
        in_specs=[pl.BlockSpec(memory_space=pltpu.SMEM), first] + [vmem] * (len(operands) - 1),
        out_specs=[vmem] * len(outs),
        scratch_shapes=list(scratch),
        cost_estimate=pl.CostEstimate(
            flops=products * 2 * SIDE**3, bytes_accessed=moved, transcendentals=0
        ),
    )(at, *operands)


def pack(at, blocks):
    def body(at, *refs):
        for t in range(N):
            refs[N][plane_back(at, t)] = refs[t][...]

    return call(body, at, blocks, [PANEL])[0]


def contract(at, blocks, own, other, dims, part=None):
    def body(at, blocks, own, other, keep, send):
        if dims == TN:
            left = blocks[...].reshape(N * SIDE, SIDE)
        else:
            left = jnp.concatenate([blocks[j] for j in range(N)], axis=1)
        one = dot(left, own[...].reshape(N * SIDE, SIDE), dims)
        two = dot(left, other[...].reshape(N * SIDE, SIDE), dims)
        same = at[2] == at[3]
        keep[...] = jnp.where(same, one, two)
        send[...] = jnp.where(same, two, one).astype(bf16)

    return call(body, at, [blocks, own, other], [WIDE, BLOCK], (), 2 * N, part)


def ordered(at, mine, beside, axis):
    same = at[2] == at[3]
    one = jnp.where(same, mine[...], beside[...])
    two = jnp.where(same, beside[...], mine[...])
    return jnp.concatenate([one, two], axis=axis)


def spread(at, mine, beside, own, other):
    def body(at, mine, beside, own, other, out):
        both = ordered(at, mine, beside, 1)

        @pl.loop(0, N, step=2)
        def _(j):
            two = pl.ds(j, 2)
            right = jnp.concatenate(
                [own[two].reshape(2 * SIDE, SIDE), other[two].reshape(2 * SIDE, SIDE)], axis=1
            )
            pair = dot(both, right, NT).astype(bf16)
            out[j] = pair[:, :SIDE]
            out[j + 1] = pair[:, SIDE:]

    return call(body, at, [mine, beside, own, other], [PANEL], (), 2 * N)[0]


def rotate_back(at, first, second, mine, beside):
    def body(at, first, second, mine, beside, out):
        both = ordered(at, mine, beside, 0)

        @pl.loop(0, N, step=2)
        def _(j):
            two = pl.ds(j, 2)
            left = jnp.concatenate(
                [first[two].reshape(2 * SIDE, SIDE), second[two].reshape(2 * SIDE, SIDE)], axis=1
            )
            out[two] = dot(left, both, NN).astype(bf16).reshape(2, SIDE, SIDE)

    return call(body, at, [first, second, mine, beside], [PANEL], (), 2 * N)[0]


def right_terms(at, row, mine, beside):
    def body(at, row, mine, beside, keep, send):
        both = ordered(at, mine, beside, 1)

        @pl.loop(0, N)
        def _(j):
            term = dot(row[j], both, TN).astype(bf16)
            keep[j] = term[:, :SIDE]
            send[j] = term[:, SIDE:]

    return call(body, at, [row, mine, beside], [PANEL, PANEL], (), 2 * N, 1)


def chip_sum(at, mine, arrived):
    def body(at, mine, arrived, *sends):
        for t in range(N):
            j = plane_on(at, t)
            sends[t][...] = (mine[j].astype(f32) + arrived[j].astype(f32)).astype(bf16)

    return call(body, at, [mine, arrived], [BLOCK] * N)


def update_step(
    gradient, first_moment, second_moment, left_factor, right_factor, left_basis, right_basis
):
    scale = 1.0 - decay_factor
    g, left, right = gradient[0], left_basis[0], right_basis[0]
    d, m = lax.axis_index("dp"), lax.axis_index("mp")
    at = jnp.stack([d >> 1, m >> 1, m & 1, d & 1]).astype(jnp.int32)

    both = lax.all_gather(
        jnp.stack([left, g]), "dp", axis=1, axis_index_groups=Z_GROUPS, tiled=True
    )
    both = both.reshape(2, N, SIDE, SIDE)
    r_block = to_swapped(right, 0)
    g_own = from_plane(g)
    g_own = pack(at, g_own)
    r_own = exchange_plane(jnp.broadcast_to(r_block, (N, SIDE, SIDE)))
    g_other = other_core(g_own)
    r_other = other_core(r_own)
    g_beside = neighbour(g)

    keep, send = contract(at, both, g_own, g_other, TN, 0)
    turned = neighbour(send)
    rotated_left = (keep + turned.astype(f32)).astype(bf16)
    rotated_left = everywhere_z(rotated_left)
    keep, send = contract(at, rotated_left, r_own, r_other, NN)
    terms = spread(at, g, g_beside, g_own, g_other)
    terms = lax.optimization_barrier((terms, keep))[0].reshape(N * SIDE, SIDE)
    left_sum = lax.psum_scatter(terms, "dp", axis_index_groups=Z_GROUPS, tiled=True)
    new_left = decay_factor * left_factor[0] + scale * left_sum.astype(f32)
    turned = neighbour(send)
    rotated = keep + turned.astype(f32)

    new_first = decay_moment * first_moment[0] + (1.0 - decay_moment) * rotated
    new_second = decay_moment * second_moment[0] + (1.0 - decay_moment) * rotated * rotated
    direction = (new_first / (jnp.sqrt(new_second) + epsilon)).astype(bf16)

    left_panel = both[0]
    first = placed(left_panel, swap)
    second = placed(left_panel, lambda d, m: swap(d, m ^ 1))
    direction_beside = other_core(direction)
    terms = rotate_back(at, first, second, direction, direction_beside)
    terms = exchange_plane(terms)
    back_left = jnp.sum(terms, axis=0, dtype=f32).astype(bf16)
    back_beside = neighbour(back_left)
    terms = spread(at, back_left, back_beside, r_own, r_other)
    terms = exchange_z(terms)
    update = jnp.sum(terms, axis=0, dtype=f32).astype(bf16)

    mine, theirs = right_terms(at, both, g, g_beside)
    theirs = other_core(theirs)
    sends = chip_sum(at, mine, theirs)
    arrived = [to_swapped(sends[t], t) for t in (6, 5, 7, 2)]
    arrived += [to_swapped(sends[t], t) for t in (4, 1, 3, 0)]
    right_sum = sum(a.astype(f32) for a in arrived)
    new_right = decay_factor * right_factor[0] + scale * right_sum
    return tuple(x[None] for x in (new_first, new_second, new_left, new_right, update))


def solution(mesh):
    in_specs = (P(None, "mp", "dp"),) * 5 + (P(None, "dp", "mp"), P(None, "mp", "dp"))
    out_specs = (P(None, "mp", "dp"),) * 5
    return jax.shard_map(
        update_step, mesh=mesh, in_specs=in_specs, out_specs=out_specs, check_vma=False
    )
```

time: 252 us -> 208 us (0.83)
  starting transfers between devices: 109 us -> 64 us
  waiting for transfers between devices: 97.1 us -> 82 us
  between operations: 0.94 us -> 14.3 us
  other arithmetic: 6.25 us -> 8.79 us
    ppermute x33 -> x19, starting transfers between devices: 66.5 us -> 34.5 us  [placed(): return lax.ppermute(x, ('dp', 'mp'), pairs)]
    ppermute x33 -> x19, waiting for transfers between devices: 48.8 us -> 17.4 us  [placed(): return lax.ppermute(x, ('dp', 'mp'), pairs)]
    all_gather x0 -> x1, waiting for transfers between devices: none -> 9.32 us  [update_step(): lax.all_gather(jnp.stack([left, g]), 'dp', axis=1, axis_index_groups=Z_GR...]
    all_to_all x5 -> x4, starting transfers between devices: 33.4 us -> 24.9 us  [exchange(): return lax.all_to_all(x, axis, 0, 0, axis_index_groups=groups, tiled=True)]
    ppermute x4, waiting for transfers between devices: 21.6 us -> 27.4 us  [neighbour(): return lax.ppermute(x, 'dp', [(d, d ^ 1) for d in range(16)])]
    ppermute x4, waiting for transfers between devices: 1.34 us -> 4.17 us  [other_core(): return lax.ppermute(x, 'mp', [(m, m ^ 1) for m in range(16)])]
    ppermute x4, starting transfers between devices: 7.48 us -> 4.65 us  [neighbour(): return lax.ppermute(x, 'dp', [(d, d ^ 1) for d in range(16)])]
    all_to_all x5 -> x4, waiting for transfers between devices: 25.4 us -> 23.5 us  [exchange(): return lax.all_to_all(x, axis, 0, 0, axis_index_groups=groups, tiled=True)]
  transfers between devices with their start and end apart: 46 -> 33, of which waited for: 20 -> 15; matrix products, arithmetic and copies ran while one was open for 3% -> 4% of each run, Pallas kernels for 10% -> 12%
where the time goes in v1:
time: 208 us; the launch traced here: 204 us
  waiting for transfers between devices  82 us (39%)
  starting transfers between devices  64 us (31%)
  Pallas kernels  28.4 us (14%)
  between operations  14.3 us (7%)
  other arithmetic  8.79 us (4%)
  local copies, waits for them, and re-layouts  7.04 us (3%)
    ppermute x19, starting transfers between devices, placed(): return lax.ppermute(x, ('dp', 'mp'), pairs)  34.5 us
    pallas_call x8, Pallas kernels, call(): pl.pallas_call(body, out_shape=outs, grid=() if part is None else (1,), i...  28.4 us
    ppermute x4, waiting for transfers between devices, neighbour(): return lax.ppermute(x, 'dp', [(d, d ^ 1) for d in range(16)])  27.4 us
    all_to_all x4, starting transfers between devices, exchange(): return lax.all_to_all(x, axis, 0, 0, axis_index_groups=groups, tiled=True)  24.9 us
    all_to_all x4, waiting for transfers between devices, exchange(): return lax.all_to_all(x, axis, 0, 0, axis_index_groups=groups, tiled=True)  23.5 us
    ppermute x19, waiting for transfers between devices, placed(): return lax.ppermute(x, ('dp', 'mp'), pairs)  17.4 us
    all_gather x1, waiting for transfers between devices, update_step(): lax.all_gather(jnp.stack([left, g]), 'dp', axis=1, axis_index_groups=Z_GR...  9.32 us
    ppermute x4, starting transfers between devices, neighbour(): return lax.ppermute(x, 'dp', [(d, d ^ 1) for d in range(16)])  4.65 us
  transfers between devices with their start and end apart: 33, of which 15 were waited for; matrix products, arithmetic and copies ran while one was open for 4% of the time, Pallas kernels for 12%

profile of v1, /device:TPU:16, one launch (start us, length us, event | category | flops | bytes accessed | tf_op | source)
XLA Modules:
  0.0 204.5 jit_solution(17347597235681606226)
XLA Ops:
  7.2 1.7 pad_maximum_fusion
  9.0 1.6 collective-permute-start
  10.5 1.5 collective-permute-start.1
  12.0 2.7 %collective-permute-start.2 = (bf16[256,256]{1,0:T(8,128)(2,1)}, bf16[256,256]{1,0:T(8,128)(2,1)S(1)}, u32[]{:S(2)}, u32[]{:S(2)}) collective-permute-start(bf16[256,256]{1,0:T(8,128)(2,1)} %bitcast.43), channel_id=1, source_target_pairs={{0,4},{1,20},{2,6},{3,22},{4,0},{5,16},{6,2},{7,18},{8,12},{9,28},... | collective-permute-start | bytes 393224 | tf_op jit(solution)/shard_map/ppermute | solution.py:45
  14.8 1.4 collective-permute-start.3
  16.2 0.3 collective-permute-start.4
  16.5 3.2 %collective-permute-start.5 = (bf16[256,256]{1,0:T(8,128)(2,1)}, bf16[256,256]{1,0:T(8,128)(2,1)S(1)}, u32[]{:S(2)}, u32[]{:S(2)}) collective-permute-start(bf16[256,256]{1,0:T(8,128)(2,1)} %bitcast.46), channel_id=1, source_target_pairs={{0,10},{1,26},{2,12},{3,28},{4,14},{5,30},{6,8},{7,24},{8,2},{9,18... | collective-permute-start | bytes 393224 | tf_op jit(solution)/shard_map/ppermute | solution.py:45
  19.8 0.8 collective-permute-start.6
  20.6 0.8 collective-permute-done.2.refs_2_
  21.4 3.4 %collective-permute-start.7 = (bf16[256,256]{1,0:T(8,128)(2,1)}, bf16[256,256]{1,0:T(8,128)(2,1)S(1)}, u32[]{:S(2)}, u32[]{:S(2)}) collective-permute-start(bf16[256,256]{1,0:T(8,128)(2,1)} %bitcast.48), channel_id=1, source_target_pairs={{0,14},{1,30},{2,8},{3,24},{4,10},{5,26},{6,12},{7,28},{8,6},{9,22... | collective-permute-start | bytes 393224 | tf_op jit(solution)/shard_map/ppermute | solution.py:45
  24.7 0.6 pad_add_fusion.at
  25.4 1.2 collective-permute-done.4.refs_4_
  26.5 4.7 %collective-permute-done.6.refs_6_ = bf16[256,256]{1,0:T(8,128)(2,1)S(1)} collective-permute-done((bf16[256,256]{1,0:T(8,128)(2,1)}, bf16[256,256]{1,0:T(8,128)(2,1)S(1)}, u32[]{:S(2)}, u32[]{:S(2)}) %collective-permute-start.6) | collective-permute-done | bytes 131104 | tf_op jit(solution)/shard_map/ppermute | solution.py:45
  31.3 1.8 collective-permute-done.7.refs_7_
  33.2 0.6 copy-done.20
  33.8 2.3 %shard_map.110.own = bf16[8,256,256]{2,1,0:T(8,128)(2,1)} custom-call(s32[4]{0:T(128)} %pad_add_fusion.at, bf16[256,256]{1,0:T(8,128)(2,1)} %copy-done.13, bf16[256,256]{1,0:T(8,128)(2,1)} %copy-done.14, bf16[256,256]{1,0:T(8,128)(2,1)} %copy-done.15, bf16[256,256]{1,0:T(8,128)(2,1)} %copy-done.16, bf16[256,256]{1,0:T(8,128)(2,1)} %copy-done.17, ...), custom_call_target="tpu_custom_call" | custom-call | bytes 2097152 | tf_op jit(solution)/shard_map/pallas_call | solution.py:104
  36.2 0.7 collective-permute-start.10
  36.9 1.0 broadcast_in_dim.22
  37.9 6.8 %all-to-all-start.1 = ((bf16[8,256,256]{2,1,0:T(8,128)(2,1)}), bf16[8,256,256]{2,1,0:T(8,128)(2,1)S(1)}, u32[]{:S(2)}, u32[]{:S(2)}) async-start(bf16[8,256,256]{2,1,0:T(8,128)(2,1)} %broadcast_in_dim.22), calls=%async_computation.1 | async-start | bytes 2097152 | tf_op jit(solution)/shard_map/all_to_all | solution.py:61
  44.7 9.3 %all-gather.2.cloned.1.call-done = bf16[2,2048,256]{2,1,0:T(8,128)(2,1)} async-done(((bf16[2,256,256]{2,1,0:T(8,128)(2,1)}), bf16[2,2048,256]{2,1,0:T(8,128)(2,1)}) %all-gather.2.cloned.1.call-update) | async-done | bytes 2097168 | tf_op jit(solution)/shard_map/all_gather | solution.py:209
  54.1 3.3 %shard_map.111 = (f32[256,256]{1,0:T(8,128)}, bf16[256,256]{1,0:T(8,128)(2,1)}) custom-call(s32[4]{0:T(128)} %pad_add_fusion.at, bf16[2,8,256,256]{3,2,1,0:T(8,128)(2,1)} %bitcast.38, bf16[8,256,256]{2,1,0:T(8,128)(2,1)} %shard_map.110.own, bf16[8,256,256]{2,1,0:T(8,128)(2,1)} %copy-done.2), custom_call_target="tpu_custom_call" | custom-call | flops 536870912 | bytes 4587520 | tf_op jit(solution)/shard_map/pallas_call | solution.py:104
  57.4 1.3 collective-permute-start.9
  58.7 4.3 %collective-permute-done.9 = bf16[256,256]{1,0:T(8,128)(2,1)S(1)} collective-permute-done((bf16[256,256]{1,0:T(8,128)(2,1)}, bf16[256,256]{1,0:T(8,128)(2,1)S(1)}, u32[]{:S(2)}, u32[]{:S(2)}) %collective-permute-start.9) | collective-permute-done | bytes 131104 | tf_op jit(solution)/shard_map/ppermute | solution.py:36
  63.0 1.0 add_convert_fusion
  64.0 1.3 broadcast_in_dim.21
  65.3 8.4 %all-to-all-start = ((bf16[8,256,256]{2,1,0:T(8,128)(2,1)}), bf16[8,256,256]{2,1,0:T(8,128)(2,1)}, u32[]{:S(2)}, u32[]{:S(2)}) async-start(bf16[8,256,256]{2,1,0:T(8,128)(2,1)} %broadcast_in_dim.21), calls=%async_computation | async-start | bytes 2097152 | tf_op jit(solution)/shard_map/all_to_all | solution.py:61
  73.7 1.0 slice.5
  74.7 2.0 collective-permute-start.23
  76.7 2.2 %collective-permute-start.24 = (bf16[8,256,256]{2,1,0:T(8,128)(2,1)}, bf16[8,256,256]{2,1,0:T(8,128)(2,1)S(1)}, u32[]{:S(2)}, u32[]{:S(2)}) collective-permute-start(bf16[8,256,256]{2,1,0:T(8,128)(2,1)} %bitcast.16), channel_id=1, source_target_pairs={{0,16},{1,0},{2,18},{3,2},{4,20},{5,4},{6,22},{7,6},{8,24},{9,8},{... | collective-permute-start | bytes 3145736 | tf_op jit(solution)/shard_map/ppermute | solution.py:45
  78.9 23.5 %all-to-all-done.blocks = bf16[8,256,256]{2,1,0:T(8,128)(2,1)} async-done(((bf16[8,256,256]{2,1,0:T(8,128)(2,1)}), bf16[8,256,256]{2,1,0:T(8,128)(2,1)}, u32[]{:S(2)}, u32[]{:S(2)}) %all-to-all-start) | async-done | bytes 1048608 | tf_op jit(solution)/shard_map/all_to_all | solution.py:61
  102.5 3.3 %shard_map.112 = (f32[256,256]{1,0:T(8,128)}, bf16[256,256]{1,0:T(8,128)(2,1)}) custom-call(s32[4]{0:T(128)} %pad_add_fusion.at, bf16[8,256,256]{2,1,0:T(8,128)(2,1)} %all-to-all-done.blocks, bf16[8,256,256]{2,1,0:T(8,128)(2,1)} %copy-done.1, bf16[8,256,256]{2,1,0:T(8,128)(2,1)} %collective-permute-done.11.other), custom_call_target="tpu_custom_call" | custom-call | flops 536870912 | bytes 3538944 | tf_op jit(solution)/shard_map/pallas_call | solution.py:104
  105.8 1.0 collective-permute-start.12
  106.8 4.7 %collective-permute-done.12 = bf16[256,256]{1,0:T(8,128)(2,1)S(1)} collective-permute-done((bf16[256,256]{1,0:T(8,128)(2,1)}, bf16[256,256]{1,0:T(8,128)(2,1)S(1)}, u32[]{:S(2)}, u32[]{:S(2)}) %collective-permute-start.12) | collective-permute-done | bytes 131104 | tf_op jit(solution)/shard_map/ppermute | solution.py:36
  111.4 2.0 divide_convert_fusion
  113.5 1.3 collective-permute-done.25.beside
  114.8 0.6 copy-done.21
  115.4 3.9 %shard_map.116 = bf16[8,256,256]{2,1,0:T(8,128)(2,1)} custom-call(s32[4]{0:T(128)} %pad_add_fusion.at, bf16[8,256,256]{2,1,0:T(8,128)(2,1)} %copy-done.5, bf16[8,256,256]{2,1,0:T(8,128)(2,1)} %copy-done.6, bf16[256,256]{1,0:T(8,128)(2,1)} %copy-done.8, bf16[256,256]{1,0:T(8,128)(2,1)} %copy-done.21), custom_call_target="tpu_custom_call" | custom-call | flops 536870912 | bytes 3407872 | tf_op jit(solution)/shard_map/pallas_call | solution.py:104
  119.3 6.2 %all-to-all-start.2 = ((bf16[8,256,256]{2,1,0:T(8,128)(2,1)}), bf16[8,256,256]{2,1,0:T(8,128)(2,1)S(1)}, u32[]{:S(2)}, u32[]{:S(2)}) async-start(bf16[8,256,256]{2,1,0:T(8,128)(2,1)} %shard_map.116), calls=%async_computation.3 | async-start | bytes 2097152 | tf_op jit(solution)/shard_map/all_to_all | solution.py:61
  125.5 1.0 collective-permute-start.13
  126.5 14.8 %collective-permute-done.13.beside = bf16[256,256]{1,0:T(8,128)(2,1)S(1)} collective-permute-done((bf16[256,256]{1,0:T(8,128)(2,1)S(1)}, bf16[256,256]{1,0:T(8,128)(2,1)S(1)}, u32[]{:S(2)}, u32[]{:S(2)}) %collective-permute-start.13) | collective-permute-done | bytes 131104 | tf_op jit(solution)/shard_map/ppermute | solution.py:36
  141.3 0.7 copy-done.7
  141.9 4.1 %shard_map.113 = bf16[8,256,256]{2,1,0:T(8,128)(2,1)} custom-call(s32[4]{0:T(128)} %pad_add_fusion.at, bf16[256,256]{1,0:T(8,128)(2,1)} %bitcast.49, bf16[256,256]{1,0:T(8,128)(2,1)} %copy-done.7, bf16[8,256,256]{2,1,0:T(8,128)(2,1)} %shard_map.110.own, bf16[8,256,256]{2,1,0:T(8,128)(2,1)} %copy-done.2), custom_call_target="tpu_custom_call" | custom-call | flops 536870912 | bytes 3407872 | tf_op jit(solution)/shard_map/pallas_call | solution.py:104
  146.0 0.1 reduce_sum.24.mine
  146.2 1.3 collective-permute-start.26
  147.5 3.7 %collective-permute-done.26.beside = bf16[256,256]{1,0:T(8,128)(2,1)S(1)} collective-permute-done((bf16[256,256]{1,0:T(8,128)(2,1)S(1)}, bf16[256,256]{1,0:T(8,128)(2,1)S(1)}, u32[]{:S(2)}, u32[]{:S(2)}) %collective-permute-start.26) | collective-permute-done | bytes 131104 | tf_op jit(solution)/shard_map/ppermute | solution.py:36
  151.2 0.7 copy-done.22
  151.9 4.0 %shard_map.117 = bf16[8,256,256]{2,1,0:T(8,128)(2,1)} custom-call(s32[4]{0:T(128)} %pad_add_fusion.at, bf16[256,256]{1,0:T(8,128)(2,1)} %copy-done.9, bf16[256,256]{1,0:T(8,128)(2,1)} %copy-done.22, bf16[8,256,256]{2,1,0:T(8,128)(2,1)} %copy-done.1, bf16[8,256,256]{2,1,0:T(8,128)(2,1)} %collective-permute-done.11.other), custom_call_target="tpu_custom_call" | custom-call | flops 536870912 | bytes 3407872 | tf_op jit(solution)/shard_map/pallas_call | solution.py:104
  155.9 3.6 %all-to-all-start.3 = ((bf16[8,256,256]{2,1,0:T(8,128)(2,1)}), bf16[8,256,256]{2,1,0:T(8,128)(2,1)S(1)}, u32[]{:S(2)}, u32[]{:S(2)}) async-start(bf16[8,256,256]{2,1,0:T(8,128)(2,1)} %shard_map.117), calls=%async_computation.4 | async-start | bytes 2097152 | tf_op jit(solution)/shard_map/all_to_all | solution.py:61
  159.5 4.8 %shard_map.114 = (bf16[8,256,256]{2,1,0:T(8,128)(2,1)}, bf16[8,256,256]{2,1,0:T(8,128)(2,1)}) custom-call(s32[4]{0:T(128)} %pad_add_fusion.at, bf16[2,8,256,256]{3,2,1,0:T(8,128)(2,1)} %bitcast.39, bf16[256,256]{1,0:T(8,128)(2,1)} %bitcast.50, bf16[256,256]{1,0:T(8,128)(2,1)} %copy-done.7), custom_call_target="tpu_custom_call" | custom-call | flops 536870912 | bytes 4456448 | tf_op jit(solution)/shard_map/pallas_call | solution.py:104
  164.3 2.9 %collective-permute-done.14.arrived = bf16[8,256,256]{2,1,0:T(8,128)(2,1)S(1)} collective-permute-done((bf16[8,256,256]{2,1,0:T(8,128)(2,1)}, bf16[8,256,256]{2,1,0:T(8,128)(2,1)S(1)}, u32[]{:S(2)}, u32[]{:S(2)}) %collective-permute-start.14) | collective-permute-done | bytes 1048608 | tf_op jit(solution)/shard_map/ppermute | solution.py:32
  167.1 1.0 copy-done.4
  168.2 2.7 %shard_map.115 = (bf16[256,256]{1,0:T(8,128)(2,1)}, bf16[256,256]{1,0:T(8,128)(2,1)}, bf16[256,256]{1,0:T(8,128)(2,1)}, bf16[256,256]{1,0:T(8,128)(2,1)}, bf16[2...) custom-call(s32[4]{0:T(128)} %pad_add_fusion.at, ...), custom_call_target="tpu_custom_call" | custom-call | bytes 3145728 | tf_op jit(solution)/shard_map/pallas_call | solution.py:104
  170.8 1.6 collective-permute-start.22
  172.4 3.2 %collective-permute-start.21 = (bf16[256,256]{1,0:T(8,128)(2,1)}, bf16[256,256]{1,0:T(8,128)(2,1)S(1)}, u32[]{:S(2)}, u32[]{:S(2)}) collective-permute-start(bf16[256,256]{1,0:T(8,128)(2,1)} %get-tuple-element.33), channel_id=1, source_target_pairs={{0,6},{1,22},{2,0},{3,16},{4,2},{5,18},{6,4},{7,20},{8,14},{9,30},... | collective-permute-start | bytes 393224 | tf_op jit(solution)/shard_map/ppermute | solution.py:45
  175.6 2.3 %collective-permute-start.18 = (bf16[256,256]{1,0:T(8,128)(2,1)}, bf16[256,256]{1,0:T(8,128)(2,1)S(1)}, u32[]{:S(2)}, u32[]{:S(2)}) collective-permute-start(bf16[256,256]{1,0:T(8,128)(2,1)} %get-tuple-element.30), channel_id=1, source_target_pairs={{0,4},{1,20},{2,6},{3,22},{4,0},{5,16},{6,2},{7,18},{8,12},{9,28},... | collective-permute-start | bytes 393224 | tf_op jit(solution)/shard_map/ppermute | solution.py:45
  177.9 3.9 %collective-permute-start.17 = (bf16[256,256]{1,0:T(8,128)(2,1)}, bf16[256,256]{1,0:T(8,128)(2,1)S(1)}, u32[]{:S(2)}, u32[]{:S(2)}) collective-permute-start(bf16[256,256]{1,0:T(8,128)(2,1)} %get-tuple-element.29), channel_id=1, source_target_pairs={{0,14},{1,30},{2,8},{3,24},{4,10},{5,26},{6,12},{7,28},{8,6},{9,22... | collective-permute-start | bytes 393224 | tf_op jit(solution)/shard_map/ppermute | solution.py:45
  181.8 0.9 collective-permute-start.16
  182.8 1.1 collective-permute-done.20
  183.9 2.7 %collective-permute-start.15 = (bf16[256,256]{1,0:T(8,128)(2,1)}, bf16[256,256]{1,0:T(8,128)(2,1)S(1)}, u32[]{:S(2)}, u32[]{:S(2)}) collective-permute-start(bf16[256,256]{1,0:T(8,128)(2,1)} %get-tuple-element.27), channel_id=1, source_target_pairs={{0,12},{1,28},{2,14},{3,30},{4,8},{5,24},{6,10},{7,26},{8,4},{9,20... | collective-permute-start | bytes 393224 | tf_op jit(solution)/shard_map/ppermute | solution.py:45
  186.6 3.2 %collective-permute-done.17 = bf16[256,256]{1,0:T(8,128)(2,1)S(1)} collective-permute-done((bf16[256,256]{1,0:T(8,128)(2,1)}, bf16[256,256]{1,0:T(8,128)(2,1)S(1)}, u32[]{:S(2)}, u32[]{:S(2)}) %collective-permute-start.17) | collective-permute-done | bytes 131104 | tf_op jit(solution)/shard_map/ppermute | solution.py:45
  189.8 4.6 %collective-permute-done.16 = bf16[256,256]{1,0:T(8,128)(2,1)S(1)} collective-permute-done((bf16[256,256]{1,0:T(8,128)(2,1)}, bf16[256,256]{1,0:T(8,128)(2,1)S(1)}, u32[]{:S(2)}, u32[]{:S(2)}) %collective-permute-start.16) | collective-permute-done | bytes 131104 | tf_op jit(solution)/shard_map/ppermute | solution.py:45
  194.3 0.9 fusion.1
  195.2 1.6 fusion.2
  196.8 0.8 reduce_sum.25
  (71 shorter events, 0.2 us)
Async XLA Ops:
  7.2 29.0 %copy-start.23 = (bf16[1,256,256]{2,1,0:T(8,128)(2,1)S(1)}, bf16[1,256,256]{2,1,0:T(8,128)(2,1)}, u32[]{:S(2)}) copy-start(bf16[1,256,256]{2,1,0:T(8,128)(2,1)} %param.13) | copy-start | bytes 393220
  7.2 46.9 %all-gather.2.cloned.1.call-start = ((), (), s32[]{:S(2)}) async-start(), calls=%async_computation.5 | async-start | bytes 2359296 | tf_op jit(solution)/shard_map/all_gather | solution.py:209
  9.0 7.6 %collective-permute-start = (bf16[256,256]{1,0:T(8,128)(2,1)}, bf16[256,256]{1,0:T(8,128)(2,1)S(1)}, u32[]{:S(2)}, u32[]{:S(2)}) collective-permute-start(bf16[256,256]{1,0:T(8,128)(2,1)} %bitcast.41), channel_id=1, source_target_pairs={{0,0},{1,16},{2,2},{3,18},{4,4},{5,20},{6,6},{7,22},{8,8},{9,24},{... | collective-permute-start | bytes 393224 | tf_op jit(solution)/shard_map/ppermute | solution.py:45
  10.5 9.2 %collective-permute-start.1 = (bf16[256,256]{1,0:T(8,128)(2,1)}, bf16[256,256]{1,0:T(8,128)(2,1)S(1)}, u32[]{:S(2)}, u32[]{:S(2)}) collective-permute-start(bf16[256,256]{1,0:T(8,128)(2,1)} %bitcast.42), channel_id=1, source_target_pairs={{0,2},{1,18},{2,4},{3,20},{4,6},{5,22},{6,0},{7,16},{8,10},{9,26},... | collective-permute-start | bytes 393224 | tf_op jit(solution)/shard_map/ppermute | solution.py:45
  12.0 9.3 %collective-permute-start.2 = (bf16[256,256]{1,0:T(8,128)(2,1)}, bf16[256,256]{1,0:T(8,128)(2,1)S(1)}, u32[]{:S(2)}, u32[]{:S(2)}) collective-permute-start(bf16[256,256]{1,0:T(8,128)(2,1)} %bitcast.43), channel_id=1, source_target_pairs={{0,4},{1,20},{2,6},{3,22},{4,0},{5,16},{6,2},{7,18},{8,12},{9,28},... | collective-permute-start | bytes 393224 | tf_op jit(solution)/shard_map/ppermute | solution.py:45
  14.8 10.6 %collective-permute-start.3 = (bf16[256,256]{1,0:T(8,128)(2,1)}, bf16[256,256]{1,0:T(8,128)(2,1)S(1)}, u32[]{:S(2)}, u32[]{:S(2)}) collective-permute-start(bf16[256,256]{1,0:T(8,128)(2,1)} %bitcast.44), channel_id=1, source_target_pairs={{0,6},{1,22},{2,0},{3,16},{4,2},{5,18},{6,4},{7,20},{8,14},{9,30},... | collective-permute-start | bytes 393224 | tf_op jit(solution)/shard_map/ppermute | solution.py:45
  16.2 10.3 %collective-permute-start.4 = (bf16[256,256]{1,0:T(8,128)(2,1)}, bf16[256,256]{1,0:T(8,128)(2,1)S(1)}, u32[]{:S(2)}, u32[]{:S(2)}) collective-permute-start(bf16[256,256]{1,0:T(8,128)(2,1)} %bitcast.45), channel_id=1, source_target_pairs={{0,8},{1,24},{2,10},{3,26},{4,12},{5,28},{6,14},{7,30},{8,0},{9,16... | collective-permute-start | bytes 393224 | tf_op jit(solution)/shard_map/ppermute | solution.py:45
  16.5 16.6 %copy-start.13 = (bf16[256,256]{1,0:T(8,128)(2,1)}, bf16[256,256]{1,0:T(8,128)(2,1)S(1)}, u32[]{:S(2)}) copy-start(bf16[256,256]{1,0:T(8,128)(2,1)S(1)} %collective-permute-done.refs_0_) | copy-start | bytes 393220
  16.5 10.0 %collective-permute-start.5 = (bf16[256,256]{1,0:T(8,128)(2,1)}, bf16[256,256]{1,0:T(8,128)(2,1)S(1)}, u32[]{:S(2)}, u32[]{:S(2)}) collective-permute-start(bf16[256,256]{1,0:T(8,128)(2,1)} %bitcast.46), channel_id=1, source_target_pairs={{0,10},{1,26},{2,12},{3,28},{4,14},{5,30},{6,8},{7,24},{8,2},{9,18... | collective-permute-start | bytes 393224 | tf_op jit(solution)/shard_map/ppermute | solution.py:45
  19.8 13.4 %copy-start.14 = (bf16[256,256]{1,0:T(8,128)(2,1)}, bf16[256,256]{1,0:T(8,128)(2,1)S(1)}, u32[]{:S(2)}) copy-start(bf16[256,256]{1,0:T(8,128)(2,1)S(1)} %collective-permute-done.1.refs_1_) | copy-start | bytes 393220
  19.8 11.5 %collective-permute-start.6 = (bf16[256,256]{1,0:T(8,128)(2,1)}, bf16[256,256]{1,0:T(8,128)(2,1)S(1)}, u32[]{:S(2)}, u32[]{:S(2)}) collective-permute-start(bf16[256,256]{1,0:T(8,128)(2,1)} %bitcast.47), channel_id=1, source_target_pairs={{0,12},{1,28},{2,14},{3,30},{4,8},{5,24},{6,10},{7,26},{8,4},{9,20... | collective-permute-start | bytes 393224 | tf_op jit(solution)/shard_map/ppermute | solution.py:45
  21.4 11.8 %copy-start.15 = (bf16[256,256]{1,0:T(8,128)(2,1)}, bf16[256,256]{1,0:T(8,128)(2,1)S(1)}, u32[]{:S(2)}) copy-start(bf16[256,256]{1,0:T(8,128)(2,1)S(1)} %collective-permute-done.2.refs_2_) | copy-start | bytes 393220
  21.4 11.8 %collective-permute-start.7 = (bf16[256,256]{1,0:T(8,128)(2,1)}, bf16[256,256]{1,0:T(8,128)(2,1)S(1)}, u32[]{:S(2)}, u32[]{:S(2)}) collective-permute-start(bf16[256,256]{1,0:T(8,128)(2,1)} %bitcast.48), channel_id=1, source_target_pairs={{0,14},{1,30},{2,8},{3,24},{4,10},{5,26},{6,12},{7,28},{8,6},{9,22... | collective-permute-start | bytes 393224 | tf_op jit(solution)/shard_map/ppermute | solution.py:45
  25.4 7.8 %copy-start.16 = (bf16[256,256]{1,0:T(8,128)(2,1)}, bf16[256,256]{1,0:T(8,128)(2,1)S(1)}, u32[]{:S(2)}) copy-start(bf16[256,256]{1,0:T(8,128)(2,1)S(1)} %collective-permute-done.3.refs_3_) | copy-start | bytes 393220
  26.5 6.6 %copy-start.17 = (bf16[256,256]{1,0:T(8,128)(2,1)}, bf16[256,256]{1,0:T(8,128)(2,1)S(1)}, u32[]{:S(2)}) copy-start(bf16[256,256]{1,0:T(8,128)(2,1)S(1)} %collective-permute-done.4.refs_4_) | copy-start | bytes 393220
  26.5 6.6 %copy-start.18 = (bf16[256,256]{1,0:T(8,128)(2,1)}, bf16[256,256]{1,0:T(8,128)(2,1)S(1)}, u32[]{:S(2)}) copy-start(bf16[256,256]{1,0:T(8,128)(2,1)S(1)} %collective-permute-done.5.refs_5_) | copy-start | bytes 393220
  31.3 1.9 copy-start.19
  33.2 0.6 copy-start.20
  36.2 8.6 %collective-permute-start.8 = (bf16[8,256,256]{2,1,0:T(8,128)(2,1)}, bf16[8,256,256]{2,1,0:T(8,128)(2,1)S(1)}, u32[]{:S(2)}, u32[]{:S(2)}) collective-permute-start(bf16[8,256,256]{2,1,0:T(8,128)(2,1)} %shard_map.110.own), channel_id=1, source_target_pairs={{0,1},{1,0},{2,3},{3,2},{4,5},{5,4},{6,7},{7,6},{8,9},{9,8},{10,11... | collective-permute-start | bytes 3145736 | tf_op jit(solution)/shard_map/ppermute | solution.py:32
  36.2 0.7 collective-permute-start.10
  37.9 26.1 %all-to-all-start.1 = ((bf16[8,256,256]{2,1,0:T(8,128)(2,1)}), bf16[8,256,256]{2,1,0:T(8,128)(2,1)S(1)}, u32[]{:S(2)}, u32[]{:S(2)}) async-start(bf16[8,256,256]{2,1,0:T(8,128)(2,1)} %broadcast_in_dim.22), calls=%async_computation.1 | async-start | bytes 2097152 | tf_op jit(solution)/shard_map/all_to_all | solution.py:61
  44.7 9.3 %copy-start.2 = (bf16[8,256,256]{2,1,0:T(8,128)(2,1)}, bf16[8,256,256]{2,1,0:T(8,128)(2,1)S(1)}, u32[]{:S(2)}) copy-start(bf16[8,256,256]{2,1,0:T(8,128)(2,1)S(1)} %collective-permute-done.8.other) | copy-start | bytes 3145732
  57.4 16.3 %copy-start = (bf16[2,2048,256]{2,1,0:T(8,128)(2,1)S(1)}, bf16[2,2048,256]{2,1,0:T(8,128)(2,1)}, u32[]{:S(2)}) copy-start(bf16[2,2048,256]{2,1,0:T(8,128)(2,1)} %all-gather.2.cloned.1.call-done) | copy-start | bytes 6291460
  57.4 5.6 %collective-permute-start.9 = (bf16[256,256]{1,0:T(8,128)(2,1)}, bf16[256,256]{1,0:T(8,128)(2,1)S(1)}, u32[]{:S(2)}, u32[]{:S(2)}) collective-permute-start(bf16[256,256]{1,0:T(8,128)(2,1)} %get-tuple-element.21), channel_id=1, source_target_pairs={{0,16},{16,0},{32,48},{48,32},{64,80},{80,64},{96,112},{112,96},{1... | collective-permute-start | bytes 393224 | tf_op jit(solution)/shard_map/ppermute | solution.py:36
  64.0 10.7 %copy-start.1 = (bf16[8,256,256]{2,1,0:T(8,128)(2,1)}, bf16[8,256,256]{2,1,0:T(8,128)(2,1)S(1)}, u32[]{:S(2)}) copy-start(bf16[8,256,256]{2,1,0:T(8,128)(2,1)S(1)} %all-to-all-done.1.own) | copy-start | bytes 3145732
  65.3 37.2 %all-to-all-start = ((bf16[8,256,256]{2,1,0:T(8,128)(2,1)}), bf16[8,256,256]{2,1,0:T(8,128)(2,1)}, u32[]{:S(2)}, u32[]{:S(2)}) async-start(bf16[8,256,256]{2,1,0:T(8,128)(2,1)} %broadcast_in_dim.21), calls=%async_computation | async-start | bytes 2097152 | tf_op jit(solution)/shard_map/all_to_all | solution.py:61
  73.6 5.3 %collective-permute-start.11 = (bf16[8,256,256]{2,1,0:T(8,128)(2,1)S(1)}, bf16[8,256,256]{2,1,0:T(8,128)(2,1)}, u32[]{:S(2)}, u32[]{:S(2)}) collective-permute-start(bf16[8,256,256]{2,1,0:T(8,128)(2,1)S(1)} %all-to-all-done.1.own), channel_id=1, source_target_pairs={{0,1},{1,0},{2,3},{3,2},{4,5},{5,4},{6,7},{7,6},{8,9},{9,8},{10,11... | collective-permute-start | bytes 3145736 | tf_op jit(solution)/shard_map/ppermute | solution.py:32
  74.7 36.7 %copy-start.11 = (f32[1,256,256]{2,1,0:T(8,128)S(1)}, f32[1,256,256]{2,1,0:T(8,128)}, u32[]{:S(2)}) copy-start(f32[1,256,256]{2,1,0:T(8,128)} %param.8) | copy-start | bytes 786436
  74.7 38.7 %collective-permute-start.23 = (bf16[8,256,256]{2,1,0:T(8,128)(2,1)}, bf16[8,256,256]{2,1,0:T(8,128)(2,1)S(1)}, u32[]{:S(2)}, u32[]{:S(2)}) collective-permute-start(bf16[8,256,256]{2,1,0:T(8,128)(2,1)} %bitcast.16), channel_id=1, source_target_pairs={{0,0},{1,16},{2,2},{3,18},{4,4},{5,20},{6,6},{7,22},{8,8},{9,24},{... | collective-permute-start | bytes 3145736 | tf_op jit(solution)/shard_map/ppermute | solution.py:45
  76.7 36.7 %collective-permute-start.24 = (bf16[8,256,256]{2,1,0:T(8,128)(2,1)}, bf16[8,256,256]{2,1,0:T(8,128)(2,1)S(1)}, u32[]{:S(2)}, u32[]{:S(2)}) collective-permute-start(bf16[8,256,256]{2,1,0:T(8,128)(2,1)} %bitcast.16), channel_id=1, source_target_pairs={{0,16},{1,0},{2,18},{3,2},{4,20},{5,4},{6,22},{7,6},{8,24},{9,8},{... | collective-permute-start | bytes 3145736 | tf_op jit(solution)/shard_map/ppermute | solution.py:45
  105.8 5.6 %collective-permute-start.12 = (bf16[256,256]{1,0:T(8,128)(2,1)}, bf16[256,256]{1,0:T(8,128)(2,1)S(1)}, u32[]{:S(2)}, u32[]{:S(2)}) collective-permute-start(bf16[256,256]{1,0:T(8,128)(2,1)} %get-tuple-element.23), channel_id=1, source_target_pairs={{0,16},{16,0},{32,48},{48,32},{64,80},{80,64},{96,112},{112,96},{1... | collective-permute-start | bytes 393224 | tf_op jit(solution)/shard_map/ppermute | solution.py:36
  113.4 1.4 copy-start.8
  113.4 12.1 %copy-start.3 = (bf16[1,256,256]{2,1,0:T(8,128)(2,1)S(1)}, bf16[1,256,256]{2,1,0:T(8,128)(2,1)}, u32[]{:S(2)}) copy-start(bf16[1,256,256]{2,1,0:T(8,128)(2,1)} %param.7) | copy-start | bytes 393220
  113.4 1.3 collective-permute-start.25
  113.4 1.3 copy-start.5
  113.4 1.3 copy-start.6
  114.8 0.7 copy-start.21
  119.3 26.7 %all-to-all-start.2 = ((bf16[8,256,256]{2,1,0:T(8,128)(2,1)}), bf16[8,256,256]{2,1,0:T(8,128)(2,1)S(1)}, u32[]{:S(2)}, u32[]{:S(2)}) async-start(bf16[8,256,256]{2,1,0:T(8,128)(2,1)} %shard_map.116), calls=%async_computation.3 | async-start | bytes 2097152 | tf_op jit(solution)/shard_map/all_to_all | solution.py:61
  125.4 69.7 %reduce-scatter.2.cloned.1.call-start = ((), (), s32[]{:S(2)}) async-start(), calls=%async_computation.6 | async-start | bytes 1179648 | tf_op jit(solution)/shard_map/reduce_scatter | solution.py:228
  125.5 15.8 %collective-permute-start.13 = (bf16[256,256]{1,0:T(8,128)(2,1)S(1)}, bf16[256,256]{1,0:T(8,128)(2,1)S(1)}, u32[]{:S(2)}, u32[]{:S(2)}) collective-permute-start(bf16[256,256]{1,0:T(8,128)(2,1)S(1)} %bitcast.51), channel_id=1, source_target_pairs={{0,16},{16,0},{32,48},{48,32},{64,80},{80,64},{96,112},{112,96},{1... | collective-permute-start | bytes 393224 | tf_op jit(solution)/shard_map/ppermute | solution.py:36
  141.3 0.7 copy-start.7
  146.2 5.1 %copy-start.9 = (bf16[256,256]{1,0:T(8,128)(2,1)}, bf16[256,256]{1,0:T(8,128)(2,1)S(1)}, u32[]{:S(2)}) copy-start(bf16[256,256]{1,0:T(8,128)(2,1)S(1)} %reduce_sum.24.mine) | copy-start | bytes 393220
  146.2 5.1 %collective-permute-start.26 = (bf16[256,256]{1,0:T(8,128)(2,1)S(1)}, bf16[256,256]{1,0:T(8,128)(2,1)S(1)}, u32[]{:S(2)}, u32[]{:S(2)}) collective-permute-start(bf16[256,256]{1,0:T(8,128)(2,1)S(1)} %reduce_sum.24.mine), channel_id=1, source_target_pairs={{0,16},{16,0},{32,48},{48,32},{64,80},{80,64},{96,112},{112,96},{1... | collective-permute-start | bytes 393224 | tf_op jit(solution)/shard_map/ppermute | solution.py:36
  151.2 0.7 copy-start.22
  155.9 40.9 %all-to-all-start.3 = ((bf16[8,256,256]{2,1,0:T(8,128)(2,1)}), bf16[8,256,256]{2,1,0:T(8,128)(2,1)S(1)}, u32[]{:S(2)}, u32[]{:S(2)}) async-start(bf16[8,256,256]{2,1,0:T(8,128)(2,1)} %shard_map.117), calls=%async_computation.4 | async-start | bytes 2097152 | tf_op jit(solution)/shard_map/all_to_all | solution.py:61
  159.5 34.8 %copy-start.12 = (f32[1,256,256]{2,1,0:T(8,128)S(1)}, f32[1,256,256]{2,1,0:T(8,128)}, u32[]{:S(2)}) copy-start(f32[1,256,256]{2,1,0:T(8,128)} %param.11) | copy-start | bytes 786436
  164.3 30.9 %copy-start.10 = (f32[1,256,256]{2,1,0:T(8,128)S(1)}, f32[1,256,256]{2,1,0:T(8,128)}, u32[]{:S(2)}) copy-start(f32[1,256,256]{2,1,0:T(8,128)} %param.10) | copy-start | bytes 786436
  164.3 2.9 %collective-permute-start.14 = (bf16[8,256,256]{2,1,0:T(8,128)(2,1)}, bf16[8,256,256]{2,1,0:T(8,128)(2,1)S(1)}, u32[]{:S(2)}, u32[]{:S(2)}) collective-permute-start(bf16[8,256,256]{2,1,0:T(8,128)(2,1)} %get-tuple-element.26), channel_id=1, source_target_pairs={{0,1},{1,0},{2,3},{3,2},{4,5},{5,4},{6,7},{7,6},{8,9},{9,8},{10,11... | collective-permute-start | bytes 3145736 | tf_op jit(solution)/shard_map/ppermute | solution.py:32
  167.1 1.0 copy-start.4
  170.8 7.1 %collective-permute-start.22 = (bf16[256,256]{1,0:T(8,128)(2,1)}, bf16[256,256]{1,0:T(8,128)(2,1)S(1)}, u32[]{:S(2)}, u32[]{:S(2)}) collective-permute-start(bf16[256,256]{1,0:T(8,128)(2,1)} %get-tuple-element.34), channel_id=1, source_target_pairs={{0,0},{1,16},{2,2},{3,18},{4,4},{5,20},{6,6},{7,22},{8,8},{9,24},{... | collective-permute-start | bytes 393224 | tf_op jit(solution)/shard_map/ppermute | solution.py:45
  172.4 9.4 %collective-permute-start.21 = (bf16[256,256]{1,0:T(8,128)(2,1)}, bf16[256,256]{1,0:T(8,128)(2,1)S(1)}, u32[]{:S(2)}, u32[]{:S(2)}) collective-permute-start(bf16[256,256]{1,0:T(8,128)(2,1)} %get-tuple-element.33), channel_id=1, source_target_pairs={{0,6},{1,22},{2,0},{3,16},{4,2},{5,18},{6,4},{7,20},{8,14},{9,30},... | collective-permute-start | bytes 393224 | tf_op jit(solution)/shard_map/ppermute | solution.py:45
  175.6 8.2 %collective-permute-start.20 = (bf16[256,256]{1,0:T(8,128)(2,1)}, bf16[256,256]{1,0:T(8,128)(2,1)S(1)}, u32[]{:S(2)}, u32[]{:S(2)}) collective-permute-start(bf16[256,256]{1,0:T(8,128)(2,1)} %get-tuple-element.32), channel_id=1, source_target_pairs={{0,2},{1,18},{2,4},{3,20},{4,6},{5,22},{6,0},{7,16},{8,10},{9,26},... | collective-permute-start | bytes 393224 | tf_op jit(solution)/shard_map/ppermute | solution.py:45
  175.6 10.9 %collective-permute-start.19 = (bf16[256,256]{1,0:T(8,128)(2,1)}, bf16[256,256]{1,0:T(8,128)(2,1)S(1)}, u32[]{:S(2)}, u32[]{:S(2)}) collective-permute-start(bf16[256,256]{1,0:T(8,128)(2,1)} %get-tuple-element.31), channel_id=1, source_target_pairs={{0,8},{1,24},{2,10},{3,26},{4,12},{5,28},{6,14},{7,30},{8,0},{9,16... | collective-permute-start | bytes 393224 | tf_op jit(solution)/shard_map/ppermute | solution.py:45
  175.6 10.9 %collective-permute-start.18 = (bf16[256,256]{1,0:T(8,128)(2,1)}, bf16[256,256]{1,0:T(8,128)(2,1)S(1)}, u32[]{:S(2)}, u32[]{:S(2)}) collective-permute-start(bf16[256,256]{1,0:T(8,128)(2,1)} %get-tuple-element.30), channel_id=1, source_target_pairs={{0,4},{1,20},{2,6},{3,22},{4,0},{5,16},{6,2},{7,18},{8,12},{9,28},... | collective-permute-start | bytes 393224 | tf_op jit(solution)/shard_map/ppermute | solution.py:45
  177.9 11.8 %collective-permute-start.17 = (bf16[256,256]{1,0:T(8,128)(2,1)}, bf16[256,256]{1,0:T(8,128)(2,1)S(1)}, u32[]{:S(2)}, u32[]{:S(2)}) collective-permute-start(bf16[256,256]{1,0:T(8,128)(2,1)} %get-tuple-element.29), channel_id=1, source_target_pairs={{0,14},{1,30},{2,8},{3,24},{4,10},{5,26},{6,12},{7,28},{8,6},{9,22... | collective-permute-start | bytes 393224 | tf_op jit(solution)/shard_map/ppermute | solution.py:45
  181.8 12.5 %collective-permute-start.16 = (bf16[256,256]{1,0:T(8,128)(2,1)}, bf16[256,256]{1,0:T(8,128)(2,1)S(1)}, u32[]{:S(2)}, u32[]{:S(2)}) collective-permute-start(bf16[256,256]{1,0:T(8,128)(2,1)} %get-tuple-element.28), channel_id=1, source_target_pairs={{0,10},{1,26},{2,12},{3,28},{4,14},{5,30},{6,8},{7,24},{8,2},{9,18... | collective-permute-start | bytes 393224 | tf_op jit(solution)/shard_map/ppermute | solution.py:45
  183.9 10.5 %collective-permute-start.15 = (bf16[256,256]{1,0:T(8,128)(2,1)}, bf16[256,256]{1,0:T(8,128)(2,1)S(1)}, u32[]{:S(2)}, u32[]{:S(2)}) collective-permute-start(bf16[256,256]{1,0:T(8,128)(2,1)} %get-tuple-element.27), channel_id=1, source_target_pairs={{0,12},{1,28},{2,14},{3,30},{4,8},{5,24},{6,10},{7,26},{8,4},{9,20... | collective-permute-start | bytes 393224 | tf_op jit(solution)/shard_map/ppermute | solution.py:45
Sparse Core Ops, SparseCore 0:
  10.3 43.6 all-gather.1
  146.1 45.4 reduce-scatter.1

commit v2 on v1

--- a/solution.py
+++ b/solution.py
@@ -26,6 +26,10 @@
 
 def back(i, t):
     return (((i >> 2) - (t >> 2)) & 1) * 4 + ((i - t) & 3)
+
+
+def along_z(x, s):
+    return lax.ppermute(x, "dp", [(d, (d + 2 * s) % 16) for d in range(16)])
 
 
 def other_core(x):
@@ -69,10 +73,6 @@
     return exchange(x, "mp", PLANE_GROUPS)
 
 
-def everywhere_z(x):
-    return exchange_z(jnp.broadcast_to(x, (N, *x.shape)))
-
-
 def from_plane(x):
     arrived = {t: to_swapped(x, t) for t in (6, 5, 7, 2, 4, 1, 3, 0)}
     return [arrived[t] for t in range(N)]
@@ -80,6 +80,10 @@
 
 def dot(a, b, dims):
     return lax.dot_general(a, b, dims, preferred_element_type=f32)
+
+
+def z_on(at, s):
+    return (at[0] + s) & 7
 
 
 def plane_back(at, t):
@@ -161,6 +165,21 @@
     return call(body, at, [mine, beside, own, other], [PANEL], (), 2 * N)[0]
 
 
+def spread_apart(at, mine, beside, own, other):
+    def body(at, mine, beside, own, other, keep, *sends):
+        both = ordered(at, mine, beside, 1)
+        for s in range(N):
+            j = z_on(at, s)
+            term = dot(both, jnp.concatenate([own[j], other[j]], axis=1), NT)
+            if s == 0:
+                keep[...] = term
+            else:
+                sends[s - 1][...] = term.astype(bf16)
+
+    outs = [WIDE] + [BLOCK] * (N - 1)
+    return call(body, at, [mine, beside, own, other], outs, (), 2 * N)
+
+
 def rotate_back(at, first, second, mine, beside):
     def body(at, first, second, mine, beside, out):
         both = ordered(at, mine, beside, 0)
@@ -221,7 +240,7 @@
     keep, send = contract(at, both, g_own, g_other, TN, 0)
     turned = neighbour(send)
     rotated_left = (keep + turned.astype(f32)).astype(bf16)
-    rotated_left = everywhere_z(rotated_left)
+    rotated_left = exchange_z(jnp.broadcast_to(rotated_left, (N, SIDE, SIDE)))
     keep, send = contract(at, rotated_left, r_own, r_other, NN)
     terms = spread(at, g, g_beside, g_own, g_other)
     terms = lax.optimization_barrier((terms, keep))[0].reshape(N * SIDE, SIDE)
@@ -242,10 +261,8 @@
     terms = exchange_plane(terms)
     back_left = jnp.sum(terms, axis=0, dtype=f32).astype(bf16)
     back_beside = neighbour(back_left)
-    terms = spread(at, back_left, back_beside, r_own, r_other)
-    terms = exchange_z(terms)
-    update = jnp.sum(terms, axis=0, dtype=f32).astype(bf16)
-
+    keep, *terms = spread_apart(at, back_left, back_beside, r_own, r_other)
+    updates = [along_z(terms[s - 1], s) for s in (4, 3, 5, 2, 6, 1, 7)]
     mine, theirs = right_terms(at, both, g, g_beside)
     theirs = other_core(theirs)
     sends = chip_sum(at, mine, theirs)
@@ -253,6 +270,8 @@
     arrived += [to_swapped(sends[t], t) for t in (4, 1, 3, 0)]
     right_sum = sum(a.astype(f32) for a in arrived)
     new_right = decay_factor * right_factor[0] + scale * right_sum
+    keep, new_left, new_right = lax.optimization_barrier((keep, new_left, new_right))
+    update = (keep + sum(a.astype(f32) for a in updates)).astype(bf16)
     return tuple(x[None] for x in (new_first, new_second, new_left, new_right, update))
 
 

time: 208 us -> 211 us (1.014)
  starting transfers between devices: 64 us -> 77.5 us
  waiting for transfers between devices: 82 us -> 72.6 us
    all_to_all x4 -> x3, waiting for transfers between devices: 23.5 us -> 4.11 us  [exchange(): return lax.all_to_all(x, axis, 0, 0, axis_index_groups=groups, tiled=True)]
    ppermute x0 -> x7, starting transfers between devices: none -> 15 us  [along_z(): return lax.ppermute(x, 'dp', [(d, (d + 2 * s) % 16) for d in range(16)])]
    ppermute x0 -> x7, waiting for transfers between devices: none -> 11.5 us  [along_z(): return lax.ppermute(x, 'dp', [(d, (d + 2 * s) % 16) for d in range(16)])]
    ppermute x4, waiting for transfers between devices: 27.4 us -> 36.5 us  [neighbour(): return lax.ppermute(x, 'dp', [(d, d ^ 1) for d in range(16)])]
    ppermute x19, waiting for transfers between devices: 17.4 us -> 11.2 us  [placed(): return lax.ppermute(x, ('dp', 'mp'), pairs)]
    ppermute x4, waiting for transfers between devices: 4.17 us -> 0.01 us  [other_core(): return lax.ppermute(x, 'mp', [(m, m ^ 1) for m in range(16)])]
    all_to_all x4 -> x3, starting transfers between devices: 24.9 us -> 21.3 us  [exchange(): return lax.all_to_all(x, axis, 0, 0, axis_index_groups=groups, tiled=True)]
    add x0 -> x2, other arithmetic: none -> 2.51 us  [the longest x1 1.65 us: update_step(): new_left = decay_factor * left_factor[0] + scale * left_sum.astype(f32)]
  transfers between devices with their start and end apart: 33 -> 39, of which waited for: 15 -> 16; matrix products, arithmetic and copies ran while one was open for 4% -> 4% of each run, Pallas kernels for 12% -> 13%
where the time goes in v2:
time: 211 us; the launch traced here: 208 us
  starting transfers between devices  77.5 us (37%)
  waiting for transfers between devices  72.6 us (34%)
  Pallas kernels  27.5 us (13%)
  between operations  14.3 us (7%)
  other arithmetic  8.65 us (4%)
  local copies, waits for them, and re-layouts  7.27 us (3%)
    ppermute x19, starting transfers between devices, placed(): return lax.ppermute(x, ('dp', 'mp'), pairs)  36.6 us
    ppermute x4, waiting for transfers between devices, neighbour(): return lax.ppermute(x, 'dp', [(d, d ^ 1) for d in range(16)])  36.5 us
    pallas_call x8, Pallas kernels, call(): pl.pallas_call(body, out_shape=outs, grid=() if part is None else (1,), i...  27.5 us
    all_to_all x3, starting transfers between devices, exchange(): return lax.all_to_all(x, axis, 0, 0, axis_index_groups=groups, tiled=True)  21.3 us
    ppermute x7, starting transfers between devices, along_z(): return lax.ppermute(x, 'dp', [(d, (d + 2 * s) % 16) for d in range(16)])  15 us
    ppermute x7, waiting for transfers between devices, along_z(): return lax.ppermute(x, 'dp', [(d, (d + 2 * s) % 16) for d in range(16)])  11.5 us
    ppermute x19, waiting for transfers between devices, placed(): return lax.ppermute(x, ('dp', 'mp'), pairs)  11.2 us
    all_gather x1, waiting for transfers between devices, update_step(): lax.all_gather(jnp.stack([left, g]), 'dp', axis=1, axis_index_groups=Z_GR...  9.28 us
  transfers between devices with their start and end apart: 39, of which 16 were waited for; matrix products, arithmetic and copies ran while one was open for 4% of the time, Pallas kernels for 13%

profile of v2, /device:TPU:16, one launch (start us, length us, event | category | flops | bytes accessed | tf_op | source)
XLA Modules:
  0.0 207.8 jit_solution(11295370427951432178)
XLA Ops:
  7.2 1.7 pad_maximum_fusion
  9.0 1.6 collective-permute-start
  10.5 1.5 collective-permute-start.1
  12.0 2.7 %collective-permute-start.2 = (bf16[256,256]{1,0:T(8,128)(2,1)}, bf16[256,256]{1,0:T(8,128)(2,1)S(1)}, u32[]{:S(2)}, u32[]{:S(2)}) collective-permute-start(bf16[256,256]{1,0:T(8,128)(2,1)} %bitcast.38), channel_id=1, source_target_pairs={{0,4},{1,20},{2,6},{3,22},{4,0},{5,16},{6,2},{7,18},{8,12},{9,28},... | collective-permute-start | bytes 393224 | tf_op jit(solution)/shard_map/ppermute | solution.py:49
  14.8 1.4 collective-permute-start.3
  16.5 3.2 %collective-permute-start.5 = (bf16[256,256]{1,0:T(8,128)(2,1)}, bf16[256,256]{1,0:T(8,128)(2,1)S(1)}, u32[]{:S(2)}, u32[]{:S(2)}) collective-permute-start(bf16[256,256]{1,0:T(8,128)(2,1)} %bitcast.41), channel_id=1, source_target_pairs={{0,10},{1,26},{2,12},{3,28},{4,14},{5,30},{6,8},{7,24},{8,2},{9,18... | collective-permute-start | bytes 393224 | tf_op jit(solution)/shard_map/ppermute | solution.py:49
  19.8 0.8 collective-permute-start.6
  20.6 0.8 collective-permute-done.2.refs_2_
  21.4 3.4 %collective-permute-start.7 = (bf16[256,256]{1,0:T(8,128)(2,1)}, bf16[256,256]{1,0:T(8,128)(2,1)S(1)}, u32[]{:S(2)}, u32[]{:S(2)}) collective-permute-start(bf16[256,256]{1,0:T(8,128)(2,1)} %bitcast.43), channel_id=1, source_target_pairs={{0,14},{1,30},{2,8},{3,24},{4,10},{5,26},{6,12},{7,28},{8,6},{9,22... | collective-permute-start | bytes 393224 | tf_op jit(solution)/shard_map/ppermute | solution.py:49
  24.7 0.6 pad_add_fusion.at
  25.3 1.2 collective-permute-done.4.refs_4_
  26.5 4.7 %collective-permute-done.6.refs_6_ = bf16[256,256]{1,0:T(8,128)(2,1)S(1)} collective-permute-done((bf16[256,256]{1,0:T(8,128)(2,1)}, bf16[256,256]{1,0:T(8,128)(2,1)S(1)}, u32[]{:S(2)}, u32[]{:S(2)}) %collective-permute-start.6) | collective-permute-done | bytes 131104 | tf_op jit(solution)/shard_map/ppermute | solution.py:49
  31.3 1.8 collective-permute-done.7.refs_7_
  33.2 0.6 copy-done.22
  33.8 2.4 %shard_map.110.own = bf16[8,256,256]{2,1,0:T(8,128)(2,1)} custom-call(s32[4]{0:T(128)} %pad_add_fusion.at, bf16[256,256]{1,0:T(8,128)(2,1)} %copy-done.14, bf16[256,256]{1,0:T(8,128)(2,1)} %copy-done.15, bf16[256,256]{1,0:T(8,128)(2,1)} %copy-done.16, bf16[256,256]{1,0:T(8,128)(2,1)} %copy-done.17, bf16[256,256]{1,0:T(8,128)(2,1)} %copy-done.18, ...), custom_call_target="tpu_custom_call" | custom-call | bytes 2097152 | tf_op jit(solution)/shard_map/pallas_call | solution.py:108
  36.2 0.7 collective-permute-start.10
  36.9 1.1 broadcast_in_dim.22
  38.0 6.8 %all-to-all-start.1 = ((bf16[8,256,256]{2,1,0:T(8,128)(2,1)}), bf16[8,256,256]{2,1,0:T(8,128)(2,1)S(1)}, u32[]{:S(2)}, u32[]{:S(2)}) async-start(bf16[8,256,256]{2,1,0:T(8,128)(2,1)} %broadcast_in_dim.22), calls=%async_computation.1 | async-start | bytes 2097152 | tf_op jit(solution)/shard_map/all_to_all | solution.py:65
  44.8 9.3 %all-gather.2.cloned.1.call-done = bf16[2,2048,256]{2,1,0:T(8,128)(2,1)} async-done(((bf16[2,256,256]{2,1,0:T(8,128)(2,1)}), bf16[2,2048,256]{2,1,0:T(8,128)(2,1)}) %all-gather.2.cloned.1.call-update) | async-done | bytes 2097168 | tf_op jit(solution)/shard_map/all_gather | solution.py:228
  54.1 3.3 %shard_map.111 = (f32[256,256]{1,0:T(8,128)}, bf16[256,256]{1,0:T(8,128)(2,1)}) custom-call(s32[4]{0:T(128)} %pad_add_fusion.at, bf16[2,8,256,256]{3,2,1,0:T(8,128)(2,1)} %bitcast.33, bf16[8,256,256]{2,1,0:T(8,128)(2,1)} %shard_map.110.own, bf16[8,256,256]{2,1,0:T(8,128)(2,1)} %copy-done.2), custom_call_target="tpu_custom_call" | custom-call | flops 536870912 | bytes 4587520 | tf_op jit(solution)/shard_map/pallas_call | solution.py:108
  57.4 1.3 collective-permute-start.9
  58.7 4.3 %collective-permute-done.9 = bf16[256,256]{1,0:T(8,128)(2,1)S(1)} collective-permute-done((bf16[256,256]{1,0:T(8,128)(2,1)}, bf16[256,256]{1,0:T(8,128)(2,1)S(1)}, u32[]{:S(2)}, u32[]{:S(2)}) %collective-permute-start.9) | collective-permute-done | bytes 131104 | tf_op jit(solution)/shard_map/ppermute | solution.py:40
  63.0 1.0 add_convert_fusion.1
  64.0 1.1 broadcast_in_dim.21
  65.2 8.5 %all-to-all-start = ((bf16[8,256,256]{2,1,0:T(8,128)(2,1)}), bf16[8,256,256]{2,1,0:T(8,128)(2,1)}, u32[]{:S(2)}, u32[]{:S(2)}) async-start(bf16[8,256,256]{2,1,0:T(8,128)(2,1)} %broadcast_in_dim.21), calls=%async_computation | async-start | bytes 2097152 | tf_op jit(solution)/shard_map/all_to_all | solution.py:65
  73.8 1.1 slice.5
  74.9 1.9 collective-permute-start.13
  76.8 2.2 %collective-permute-start.14 = (bf16[8,256,256]{2,1,0:T(8,128)(2,1)}, bf16[8,256,256]{2,1,0:T(8,128)(2,1)}, u32[]{:S(2)}, u32[]{:S(2)}) collective-permute-start(bf16[8,256,256]{2,1,0:T(8,128)(2,1)} %bitcast.11), channel_id=1, source_target_pairs={{0,16},{1,0},{2,18},{3,2},{4,20},{5,4},{6,22},{7,6},{8,24},{9,8},{... | collective-permute-start | bytes 3145736 | tf_op jit(solution)/shard_map/ppermute | solution.py:49
  79.2 26.7 %collective-permute-done.17.beside = bf16[256,256]{1,0:T(8,128)(2,1)S(1)} collective-permute-done((bf16[256,256]{1,0:T(8,128)(2,1)S(1)}, bf16[256,256]{1,0:T(8,128)(2,1)S(1)}, u32[]{:S(2)}, u32[]{:S(2)}) %collective-permute-start.17) | collective-permute-done | bytes 131104 | tf_op jit(solution)/shard_map/ppermute | solution.py:40
  105.9 0.7 copy-done.7
  106.5 4.1 %shard_map.115 = bf16[8,256,256]{2,1,0:T(8,128)(2,1)} custom-call(s32[4]{0:T(128)} %pad_add_fusion.at, bf16[256,256]{1,0:T(8,128)(2,1)} %bitcast.44, bf16[256,256]{1,0:T(8,128)(2,1)} %copy-done.7, bf16[8,256,256]{2,1,0:T(8,128)(2,1)} %shard_map.110.own, bf16[8,256,256]{2,1,0:T(8,128)(2,1)} %copy-done.2), custom_call_target="tpu_custom_call" | custom-call | flops 536870912 | bytes 3407872 | tf_op jit(solution)/shard_map/pallas_call | solution.py:108
  110.6 3.4 %shard_map.112 = (f32[256,256]{1,0:T(8,128)}, bf16[256,256]{1,0:T(8,128)(2,1)}) custom-call(s32[4]{0:T(128)} %pad_add_fusion.at, bf16[8,256,256]{2,1,0:T(8,128)(2,1)} %all-to-all-done.blocks, bf16[8,256,256]{2,1,0:T(8,128)(2,1)} %copy-done.1, bf16[8,256,256]{2,1,0:T(8,128)(2,1)} %collective-permute-done.11.other), custom_call_target="tpu_custom_call" | custom-call | flops 536870912 | bytes 3538944 | tf_op jit(solution)/shard_map/pallas_call | solution.py:108
  114.3 5.4 %collective-permute-done.12 = bf16[256,256]{1,0:T(8,128)(2,1)S(1)} collective-permute-done((bf16[256,256]{1,0:T(8,128)(2,1)}, bf16[256,256]{1,0:T(8,128)(2,1)S(1)}, u32[]{:S(2)}, u32[]{:S(2)}) %collective-permute-start.12) | collective-permute-done | bytes 131104 | tf_op jit(solution)/shard_map/ppermute | solution.py:40
  119.7 1.9 divide_convert_fusion
  121.6 4.7 %shard_map.116 = (bf16[8,256,256]{2,1,0:T(8,128)(2,1)}, bf16[8,256,256]{2,1,0:T(8,128)(2,1)}) custom-call(s32[4]{0:T(128)} %pad_add_fusion.at, bf16[2,8,256,256]{3,2,1,0:T(8,128)(2,1)} %bitcast.34, bf16[256,256]{1,0:T(8,128)(2,1)} %bitcast.45, bf16[256,256]{1,0:T(8,128)(2,1)} %copy-done.7), custom_call_target="tpu_custom_call" | custom-call | flops 536870912 | bytes 4456448 | tf_op jit(solution)/shard_map/pallas_call | solution.py:108
  126.8 1.0 copy-done.5
  127.8 0.7 copy-done.23
  128.4 3.8 %shard_map.113 = bf16[8,256,256]{2,1,0:T(8,128)(2,1)} custom-call(s32[4]{0:T(128)} %pad_add_fusion.at, bf16[8,256,256]{2,1,0:T(8,128)(2,1)} %copy-done.5, bf16[8,256,256]{2,1,0:T(8,128)(2,1)} %collective-permute-done.14.second, bf16[256,256]{1,0:T(8,128)(2,1)} %copy-done.8, bf16[256,256]{1,0:T(8,128)(2,1)} %copy-done.23), custom_call_target="tpu_custom_call" | custom-call | flops 536870912 | bytes 3407872 | tf_op jit(solution)/shard_map/pallas_call | solution.py:108
  132.3 6.0 %all-to-all-start.2 = ((bf16[8,256,256]{2,1,0:T(8,128)(2,1)}), bf16[8,256,256]{2,1,0:T(8,128)(2,1)S(1)}, u32[]{:S(2)}, u32[]{:S(2)}) async-start(bf16[8,256,256]{2,1,0:T(8,128)(2,1)} %shard_map.113), calls=%async_computation.2 | async-start | bytes 2097152 | tf_op jit(solution)/shard_map/all_to_all | solution.py:65
  138.3 1.0 copy-done.4
  139.2 2.7 %shard_map.117 = (bf16[256,256]{1,0:T(8,128)(2,1)}, bf16[256,256]{1,0:T(8,128)(2,1)}, bf16[256,256]{1,0:T(8,128)(2,1)}, bf16[256,256]{1,0:T(8,128)(2,1)}, bf16[2...) custom-call(s32[4]{0:T(128)} %pad_add_fusion.at, ...), custom_call_target="tpu_custom_call" | custom-call | bytes 3145728 | tf_op jit(solution)/shard_map/pallas_call | solution.py:108
  141.9 3.0 %collective-permute-start.19 = (bf16[256,256]{1,0:T(8,128)(2,1)}, bf16[256,256]{1,0:T(8,128)(2,1)S(1)}, u32[]{:S(2)}, u32[]{:S(2)}) collective-permute-start(bf16[256,256]{1,0:T(8,128)(2,1)} %get-tuple-element.39), channel_id=1, source_target_pairs={{0,12},{1,28},{2,14},{3,30},{4,8},{5,24},{6,10},{7,26},{8,4},{9,20... | collective-permute-start | bytes 393224 | tf_op jit(solution)/shard_map/ppermute | solution.py:49
  144.9 3.0 %collective-permute-start.20 = (bf16[256,256]{1,0:T(8,128)(2,1)}, bf16[256,256]{1,0:T(8,128)(2,1)S(1)}, u32[]{:S(2)}, u32[]{:S(2)}) collective-permute-start(bf16[256,256]{1,0:T(8,128)(2,1)} %get-tuple-element.40), channel_id=1, source_target_pairs={{0,10},{1,26},{2,12},{3,28},{4,14},{5,30},{6,8},{7,24},{8,2},{9,18... | collective-permute-start | bytes 393224 | tf_op jit(solution)/shard_map/ppermute | solution.py:49
  147.9 2.7 %collective-permute-start.21 = (bf16[256,256]{1,0:T(8,128)(2,1)}, bf16[256,256]{1,0:T(8,128)(2,1)S(1)}, u32[]{:S(2)}, u32[]{:S(2)}) collective-permute-start(bf16[256,256]{1,0:T(8,128)(2,1)} %get-tuple-element.41), channel_id=1, source_target_pairs={{0,14},{1,30},{2,8},{3,24},{4,10},{5,26},{6,12},{7,28},{8,6},{9,22... | collective-permute-start | bytes 393224 | tf_op jit(solution)/shard_map/ppermute | solution.py:49
  150.5 4.1 %all-to-all-done.2 = bf16[8,256,256]{2,1,0:T(8,128)(2,1)S(1)} async-done(((bf16[8,256,256]{2,1,0:T(8,128)(2,1)}), bf16[8,256,256]{2,1,0:T(8,128)(2,1)S(1)}, u32[]{:S(2)}, u32[]{:S(2)}) %all-to-all-start.2) | async-done | bytes 1048608 | tf_op jit(solution)/shard_map/all_to_all | solution.py:65
  154.8 2.3 %collective-permute-start.16 = (bf16[256,256]{1,0:T(8,128)(2,1)S(1)}, bf16[256,256]{1,0:T(8,128)(2,1)S(1)}, u32[]{:S(2)}, u32[]{:S(2)}) collective-permute-start(bf16[256,256]{1,0:T(8,128)(2,1)S(1)} %reduce_sum.12.mine), channel_id=1, source_target_pairs={{0,16},{16,0},{32,48},{48,32},{64,80},{80,64},{96,112},{112,96},{1... | collective-permute-start | bytes 393224 | tf_op jit(solution)/shard_map/ppermute | solution.py:40
  157.1 2.6 %collective-permute-done.19 = bf16[256,256]{1,0:T(8,128)(2,1)S(1)} collective-permute-done((bf16[256,256]{1,0:T(8,128)(2,1)}, bf16[256,256]{1,0:T(8,128)(2,1)S(1)}, u32[]{:S(2)}, u32[]{:S(2)}) %collective-permute-start.19) | collective-permute-done | bytes 131104 | tf_op jit(solution)/shard_map/ppermute | solution.py:49
  159.7 3.5 %collective-permute-start.23 = (bf16[256,256]{1,0:T(8,128)(2,1)}, bf16[256,256]{1,0:T(8,128)(2,1)S(1)}, u32[]{:S(2)}, u32[]{:S(2)}) collective-permute-start(bf16[256,256]{1,0:T(8,128)(2,1)} %get-tuple-element.43), channel_id=1, source_target_pairs={{0,8},{1,24},{2,10},{3,26},{4,12},{5,28},{6,14},{7,30},{8,0},{9,16... | collective-permute-start | bytes 393224 | tf_op jit(solution)/shard_map/ppermute | solution.py:49
  163.2 1.0 collective-permute-start.24
  164.2 2.3 %collective-permute-start.25 = (bf16[256,256]{1,0:T(8,128)(2,1)}, bf16[256,256]{1,0:T(8,128)(2,1)S(1)}, u32[]{:S(2)}, u32[]{:S(2)}) collective-permute-start(bf16[256,256]{1,0:T(8,128)(2,1)} %get-tuple-element.45), channel_id=1, source_target_pairs={{0,6},{1,22},{2,0},{3,16},{4,2},{5,18},{6,4},{7,20},{8,14},{9,30},... | collective-permute-start | bytes 393224 | tf_op jit(solution)/shard_map/ppermute | solution.py:49
  166.4 1.6 collective-permute-start.26
  168.0 3.2 %shard_map.114 = (f32[256,256]{1,0:T(8,128)}, bf16[256,256]{1,0:T(8,128)(2,1)}, bf16[256,256]{1,0:T(8,128)(2,1)}, bf16[256,256]{1,0:T(8,128)(2,1)}, bf16[256,256...) custom-call(s32[4]{0:T(128)} %pad_add_fusion.at, ...), custom_call_target="tpu_custom_call" | custom-call | flops 536870912 | bytes 3538944 | tf_op jit(solution)/shard_map/pallas_call | solution.py:108
  171.2 5.8 %collective-permute-start.27 = (bf16[256,256]{1,0:T(8,128)(2,1)}, bf16[256,256]{1,0:T(8,128)(2,1)S(1)}, u32[]{:S(2)}, u32[]{:S(2)}) collective-permute-start(bf16[256,256]{1,0:T(8,128)(2,1)} %get-tuple-element.50), channel_id=1, source_target_pairs={{0,128},{16,144},{32,160},{48,176},{64,192},{80,208},{96,224},{112... | collective-permute-start | bytes 393224 | tf_op jit(solution)/shard_map/ppermute | solution.py:32
  177.0 0.6 collective-permute-start.28
  177.7 0.9 bitcast_add_fusion
  178.5 4.4 %collective-permute-start.29 = (bf16[256,256]{1,0:T(8,128)(2,1)}, bf16[256,256]{1,0:T(8,128)(2,1)S(1)}, u32[]{:S(2)}, u32[]{:S(2)}) collective-permute-start(bf16[256,256]{1,0:T(8,128)(2,1)} %get-tuple-element.52), channel_id=1, source_target_pairs={{0,160},{16,176},{32,192},{48,208},{64,224},{80,240},{96,0},{112,1... | collective-permute-start | bytes 393224 | tf_op jit(solution)/shard_map/ppermute | solution.py:32
  182.9 0.6 collective-permute-start.30
  183.5 3.5 %collective-permute-start.31 = (bf16[256,256]{1,0:T(8,128)(2,1)}, bf16[256,256]{1,0:T(8,128)(2,1)S(1)}, u32[]{:S(2)}, u32[]{:S(2)}) collective-permute-start(bf16[256,256]{1,0:T(8,128)(2,1)} %get-tuple-element.54), channel_id=1, source_target_pairs={{0,192},{16,208},{32,224},{48,240},{64,0},{80,16},{96,32},{112,48}... | collective-permute-start | bytes 393224 | tf_op jit(solution)/shard_map/ppermute | solution.py:32
  187.1 0.9 collective-permute-done.27
  188.0 5.5 %collective-permute-done.28 = bf16[256,256]{1,0:T(8,128)(2,1)S(1)} collective-permute-done((bf16[256,256]{1,0:T(8,128)(2,1)}, bf16[256,256]{1,0:T(8,128)(2,1)S(1)}, u32[]{:S(2)}, u32[]{:S(2)}) %collective-permute-start.28) | collective-permute-done | bytes 131104 | tf_op jit(solution)/shard_map/ppermute | solution.py:32
  193.5 1.6 bitcast_add_fusion.1
  195.1 2.8 %collective-permute-done.30 = bf16[256,256]{1,0:T(8,128)(2,1)S(1)} collective-permute-done((bf16[256,256]{1,0:T(8,128)(2,1)}, bf16[256,256]{1,0:T(8,128)(2,1)S(1)}, u32[]{:S(2)}, u32[]{:S(2)}) %collective-permute-start.30) | collective-permute-done | bytes 131104 | tf_op jit(solution)/shard_map/ppermute | solution.py:32
  198.1 1.7 collective-permute-done.32
  200.2 0.8 fusion.1
  (85 shorter events, 2.2 us)
Async XLA Ops:
  7.2 29.0 %copy-start.24 = (bf16[1,256,256]{2,1,0:T(8,128)(2,1)S(1)}, bf16[1,256,256]{2,1,0:T(8,128)(2,1)}, u32[]{:S(2)}) copy-start(bf16[1,256,256]{2,1,0:T(8,128)(2,1)} %param.13) | copy-start | bytes 393220
  7.2 46.9 %all-gather.2.cloned.1.call-start = ((), (), s32[]{:S(2)}) async-start(), calls=%async_computation.4 | async-start | bytes 2359296 | tf_op jit(solution)/shard_map/all_gather | solution.py:228
  9.0 7.6 %collective-permute-start = (bf16[256,256]{1,0:T(8,128)(2,1)}, bf16[256,256]{1,0:T(8,128)(2,1)S(1)}, u32[]{:S(2)}, u32[]{:S(2)}) collective-permute-start(bf16[256,256]{1,0:T(8,128)(2,1)} %bitcast.36), channel_id=1, source_target_pairs={{0,0},{1,16},{2,2},{3,18},{4,4},{5,20},{6,6},{7,22},{8,8},{9,24},{... | collective-permute-start | bytes 393224 | tf_op jit(solution)/shard_map/ppermute | solution.py:49
  10.5 9.2 %collective-permute-start.1 = (bf16[256,256]{1,0:T(8,128)(2,1)}, bf16[256,256]{1,0:T(8,128)(2,1)S(1)}, u32[]{:S(2)}, u32[]{:S(2)}) collective-permute-start(bf16[256,256]{1,0:T(8,128)(2,1)} %bitcast.37), channel_id=1, source_target_pairs={{0,2},{1,18},{2,4},{3,20},{4,6},{5,22},{6,0},{7,16},{8,10},{9,26},... | collective-permute-start | bytes 393224 | tf_op jit(solution)/shard_map/ppermute | solution.py:49
  12.0 9.3 %collective-permute-start.2 = (bf16[256,256]{1,0:T(8,128)(2,1)}, bf16[256,256]{1,0:T(8,128)(2,1)S(1)}, u32[]{:S(2)}, u32[]{:S(2)}) collective-permute-start(bf16[256,256]{1,0:T(8,128)(2,1)} %bitcast.38), channel_id=1, source_target_pairs={{0,4},{1,20},{2,6},{3,22},{4,0},{5,16},{6,2},{7,18},{8,12},{9,28},... | collective-permute-start | bytes 393224 | tf_op jit(solution)/shard_map/ppermute | solution.py:49
  14.8 10.6 %collective-permute-start.3 = (bf16[256,256]{1,0:T(8,128)(2,1)}, bf16[256,256]{1,0:T(8,128)(2,1)S(1)}, u32[]{:S(2)}, u32[]{:S(2)}) collective-permute-start(bf16[256,256]{1,0:T(8,128)(2,1)} %bitcast.39), channel_id=1, source_target_pairs={{0,6},{1,22},{2,0},{3,16},{4,2},{5,18},{6,4},{7,20},{8,14},{9,30},... | collective-permute-start | bytes 393224 | tf_op jit(solution)/shard_map/ppermute | solution.py:49
  16.2 10.3 %collective-permute-start.4 = (bf16[256,256]{1,0:T(8,128)(2,1)}, bf16[256,256]{1,0:T(8,128)(2,1)S(1)}, u32[]{:S(2)}, u32[]{:S(2)}) collective-permute-start(bf16[256,256]{1,0:T(8,128)(2,1)} %bitcast.40), channel_id=1, source_target_pairs={{0,8},{1,24},{2,10},{3,26},{4,12},{5,28},{6,14},{7,30},{8,0},{9,16... | collective-permute-start | bytes 393224 | tf_op jit(solution)/shard_map/ppermute | solution.py:49
  16.5 16.6 %copy-start.14 = (bf16[256,256]{1,0:T(8,128)(2,1)}, bf16[256,256]{1,0:T(8,128)(2,1)S(1)}, u32[]{:S(2)}) copy-start(bf16[256,256]{1,0:T(8,128)(2,1)S(1)} %collective-permute-done.refs_0_) | copy-start | bytes 393220
  16.5 10.0 %collective-permute-start.5 = (bf16[256,256]{1,0:T(8,128)(2,1)}, bf16[256,256]{1,0:T(8,128)(2,1)S(1)}, u32[]{:S(2)}, u32[]{:S(2)}) collective-permute-start(bf16[256,256]{1,0:T(8,128)(2,1)} %bitcast.41), channel_id=1, source_target_pairs={{0,10},{1,26},{2,12},{3,28},{4,14},{5,30},{6,8},{7,24},{8,2},{9,18... | collective-permute-start | bytes 393224 | tf_op jit(solution)/shard_map/ppermute | solution.py:49
  19.8 13.4 %copy-start.15 = (bf16[256,256]{1,0:T(8,128)(2,1)}, bf16[256,256]{1,0:T(8,128)(2,1)S(1)}, u32[]{:S(2)}) copy-start(bf16[256,256]{1,0:T(8,128)(2,1)S(1)} %collective-permute-done.1.refs_1_) | copy-start | bytes 393220
  19.8 11.5 %collective-permute-start.6 = (bf16[256,256]{1,0:T(8,128)(2,1)}, bf16[256,256]{1,0:T(8,128)(2,1)S(1)}, u32[]{:S(2)}, u32[]{:S(2)}) collective-permute-start(bf16[256,256]{1,0:T(8,128)(2,1)} %bitcast.42), channel_id=1, source_target_pairs={{0,12},{1,28},{2,14},{3,30},{4,8},{5,24},{6,10},{7,26},{8,4},{9,20... | collective-permute-start | bytes 393224 | tf_op jit(solution)/shard_map/ppermute | solution.py:49
  21.4 11.8 %copy-start.16 = (bf16[256,256]{1,0:T(8,128)(2,1)}, bf16[256,256]{1,0:T(8,128)(2,1)S(1)}, u32[]{:S(2)}) copy-start(bf16[256,256]{1,0:T(8,128)(2,1)S(1)} %collective-permute-done.2.refs_2_) | copy-start | bytes 393220
  21.4 11.8 %collective-permute-start.7 = (bf16[256,256]{1,0:T(8,128)(2,1)}, bf16[256,256]{1,0:T(8,128)(2,1)S(1)}, u32[]{:S(2)}, u32[]{:S(2)}) collective-permute-start(bf16[256,256]{1,0:T(8,128)(2,1)} %bitcast.43), channel_id=1, source_target_pairs={{0,14},{1,30},{2,8},{3,24},{4,10},{5,26},{6,12},{7,28},{8,6},{9,22... | collective-permute-start | bytes 393224 | tf_op jit(solution)/shard_map/ppermute | solution.py:49
  25.3 7.8 %copy-start.17 = (bf16[256,256]{1,0:T(8,128)(2,1)}, bf16[256,256]{1,0:T(8,128)(2,1)S(1)}, u32[]{:S(2)}) copy-start(bf16[256,256]{1,0:T(8,128)(2,1)S(1)} %collective-permute-done.3.refs_3_) | copy-start | bytes 393220
  26.5 6.6 %copy-start.18 = (bf16[256,256]{1,0:T(8,128)(2,1)}, bf16[256,256]{1,0:T(8,128)(2,1)S(1)}, u32[]{:S(2)}) copy-start(bf16[256,256]{1,0:T(8,128)(2,1)S(1)} %collective-permute-done.4.refs_4_) | copy-start | bytes 393220
  26.5 6.6 %copy-start.19 = (bf16[256,256]{1,0:T(8,128)(2,1)}, bf16[256,256]{1,0:T(8,128)(2,1)S(1)}, u32[]{:S(2)}) copy-start(bf16[256,256]{1,0:T(8,128)(2,1)S(1)} %collective-permute-done.5.refs_5_) | copy-start | bytes 393220
  31.3 1.9 copy-start.20
  33.2 0.6 copy-start.22
  36.2 8.6 %collective-permute-start.8 = (bf16[8,256,256]{2,1,0:T(8,128)(2,1)}, bf16[8,256,256]{2,1,0:T(8,128)(2,1)S(1)}, u32[]{:S(2)}, u32[]{:S(2)}) collective-permute-start(bf16[8,256,256]{2,1,0:T(8,128)(2,1)} %shard_map.110.own), channel_id=1, source_target_pairs={{0,1},{1,0},{2,3},{3,2},{4,5},{5,4},{6,7},{7,6},{8,9},{9,8},{10,11... | collective-permute-start | bytes 3145736 | tf_op jit(solution)/shard_map/ppermute | solution.py:36
  36.2 0.7 collective-permute-start.10
  38.0 26.1 %all-to-all-start.1 = ((bf16[8,256,256]{2,1,0:T(8,128)(2,1)}), bf16[8,256,256]{2,1,0:T(8,128)(2,1)S(1)}, u32[]{:S(2)}, u32[]{:S(2)}) async-start(bf16[8,256,256]{2,1,0:T(8,128)(2,1)} %broadcast_in_dim.22), calls=%async_computation.1 | async-start | bytes 2097152 | tf_op jit(solution)/shard_map/all_to_all | solution.py:65
  44.8 9.3 %copy-start.2 = (bf16[8,256,256]{2,1,0:T(8,128)(2,1)}, bf16[8,256,256]{2,1,0:T(8,128)(2,1)S(1)}, u32[]{:S(2)}) copy-start(bf16[8,256,256]{2,1,0:T(8,128)(2,1)S(1)} %collective-permute-done.8.other) | copy-start | bytes 3145732
  57.4 16.4 %copy-start = (bf16[2,2048,256]{2,1,0:T(8,128)(2,1)S(1)}, bf16[2,2048,256]{2,1,0:T(8,128)(2,1)}, u32[]{:S(2)}) copy-start(bf16[2,2048,256]{2,1,0:T(8,128)(2,1)} %all-gather.2.cloned.1.call-done) | copy-start | bytes 6291460
  57.4 5.6 %collective-permute-start.9 = (bf16[256,256]{1,0:T(8,128)(2,1)}, bf16[256,256]{1,0:T(8,128)(2,1)S(1)}, u32[]{:S(2)}, u32[]{:S(2)}) collective-permute-start(bf16[256,256]{1,0:T(8,128)(2,1)} %get-tuple-element.32), channel_id=1, source_target_pairs={{0,16},{16,0},{32,48},{48,32},{64,80},{80,64},{96,112},{112,96},{1... | collective-permute-start | bytes 393224 | tf_op jit(solution)/shard_map/ppermute | solution.py:40
  64.0 10.9 %copy-start.1 = (bf16[8,256,256]{2,1,0:T(8,128)(2,1)}, bf16[8,256,256]{2,1,0:T(8,128)(2,1)S(1)}, u32[]{:S(2)}) copy-start(bf16[8,256,256]{2,1,0:T(8,128)(2,1)S(1)} %all-to-all-done.1.own) | copy-start | bytes 3145732
  65.2 13.9 %copy-start.3 = (bf16[1,256,256]{2,1,0:T(8,128)(2,1)S(1)}, bf16[1,256,256]{2,1,0:T(8,128)(2,1)}, u32[]{:S(2)}) copy-start(bf16[1,256,256]{2,1,0:T(8,128)(2,1)} %param.7) | copy-start | bytes 393220
  65.2 45.4 %all-to-all-start = ((bf16[8,256,256]{2,1,0:T(8,128)(2,1)}), bf16[8,256,256]{2,1,0:T(8,128)(2,1)}, u32[]{:S(2)}, u32[]{:S(2)}) async-start(bf16[8,256,256]{2,1,0:T(8,128)(2,1)} %broadcast_in_dim.21), calls=%async_computation | async-start | bytes 2097152 | tf_op jit(solution)/shard_map/all_to_all | solution.py:65
  73.7 119.8 %reduce-scatter.2.cloned.1.call-start = ((), (), s32[]{:S(2)}) async-start(), calls=%async_computation.5 | async-start | bytes 1179648 | tf_op jit(solution)/shard_map/reduce_scatter | solution.py:247
  73.7 36.9 %collective-permute-start.11 = (bf16[8,256,256]{2,1,0:T(8,128)(2,1)S(1)}, bf16[8,256,256]{2,1,0:T(8,128)(2,1)}, u32[]{:S(2)}, u32[]{:S(2)}) collective-permute-start(bf16[8,256,256]{2,1,0:T(8,128)(2,1)S(1)} %all-to-all-done.1.own), channel_id=1, source_target_pairs={{0,1},{1,0},{2,3},{3,2},{4,5},{5,4},{6,7},{7,6},{8,9},{9,8},{10,11... | collective-permute-start | bytes 3145736 | tf_op jit(solution)/shard_map/ppermute | solution.py:36
  74.9 51.8 %collective-permute-start.13 = (bf16[8,256,256]{2,1,0:T(8,128)(2,1)}, bf16[8,256,256]{2,1,0:T(8,128)(2,1)S(1)}, u32[]{:S(2)}, u32[]{:S(2)}) collective-permute-start(bf16[8,256,256]{2,1,0:T(8,128)(2,1)} %bitcast.11), channel_id=1, source_target_pairs={{0,0},{1,16},{2,2},{3,18},{4,4},{5,20},{6,6},{7,22},{8,8},{9,24},{... | collective-permute-start | bytes 3145736 | tf_op jit(solution)/shard_map/ppermute | solution.py:49
  76.8 50.0 %collective-permute-start.14 = (bf16[8,256,256]{2,1,0:T(8,128)(2,1)}, bf16[8,256,256]{2,1,0:T(8,128)(2,1)}, u32[]{:S(2)}, u32[]{:S(2)}) collective-permute-start(bf16[8,256,256]{2,1,0:T(8,128)(2,1)} %bitcast.11), channel_id=1, source_target_pairs={{0,16},{1,0},{2,18},{3,2},{4,20},{5,4},{6,22},{7,6},{8,24},{9,8},{... | collective-permute-start | bytes 3145736 | tf_op jit(solution)/shard_map/ppermute | solution.py:49
  79.1 26.8 %collective-permute-start.17 = (bf16[256,256]{1,0:T(8,128)(2,1)S(1)}, bf16[256,256]{1,0:T(8,128)(2,1)S(1)}, u32[]{:S(2)}, u32[]{:S(2)}) collective-permute-start(bf16[256,256]{1,0:T(8,128)(2,1)S(1)} %bitcast.46), channel_id=1, source_target_pairs={{0,16},{16,0},{32,48},{48,32},{64,80},{80,64},{96,112},{112,96},{1... | collective-permute-start | bytes 393224 | tf_op jit(solution)/shard_map/ppermute | solution.py:40
  105.9 0.7 copy-start.7
  110.6 9.1 %copy-start.11 = (f32[1,256,256]{2,1,0:T(8,128)S(1)}, f32[1,256,256]{2,1,0:T(8,128)}, u32[]{:S(2)}) copy-start(f32[1,256,256]{2,1,0:T(8,128)} %param.8) | copy-start | bytes 786436
  110.6 9.1 %copy-start.12 = (f32[1,256,256]{2,1,0:T(8,128)S(1)}, f32[1,256,256]{2,1,0:T(8,128)}, u32[]{:S(2)}) copy-start(f32[1,256,256]{2,1,0:T(8,128)} %param.9) | copy-start | bytes 786436
  114.0 5.7 %collective-permute-start.12 = (bf16[256,256]{1,0:T(8,128)(2,1)}, bf16[256,256]{1,0:T(8,128)(2,1)S(1)}, u32[]{:S(2)}, u32[]{:S(2)}) collective-permute-start(bf16[256,256]{1,0:T(8,128)(2,1)} %get-tuple-element.34), channel_id=1, source_target_pairs={{0,16},{16,0},{32,48},{48,32},{64,80},{80,64},{96,112},{112,96},{1... | collective-permute-start | bytes 393224 | tf_op jit(solution)/shard_map/ppermute | solution.py:40
  121.6 5.2 %copy-start.8 = (bf16[256,256]{1,0:T(8,128)(2,1)}, bf16[256,256]{1,0:T(8,128)(2,1)S(1)}, u32[]{:S(2)}) copy-start(bf16[256,256]{1,0:T(8,128)(2,1)S(1)} %get-tuple-element.57.mine) | copy-start | bytes 393220
  121.6 5.2 %collective-permute-start.15 = (bf16[256,256]{1,0:T(8,128)(2,1)S(1)}, bf16[256,256]{1,0:T(8,128)(2,1)S(1)}, u32[]{:S(2)}, u32[]{:S(2)}) collective-permute-start(bf16[256,256]{1,0:T(8,128)(2,1)S(1)} %get-tuple-element.57.mine), channel_id=1, source_target_pairs={{0,1},{1,0},{2,3},{3,2},{4,5},{5,4},{6,7},{7,6},{8,9},{9,8},{10,11... | collective-permute-start | bytes 393224 | tf_op jit(solution)/shard_map/ppermute | solution.py:36
  126.3 11.9 %collective-permute-start.18 = (bf16[8,256,256]{2,1,0:T(8,128)(2,1)}, bf16[8,256,256]{2,1,0:T(8,128)(2,1)S(1)}, u32[]{:S(2)}, u32[]{:S(2)}) collective-permute-start(bf16[8,256,256]{2,1,0:T(8,128)(2,1)} %get-tuple-element.38), channel_id=1, source_target_pairs={{0,1},{1,0},{2,3},{3,2},{4,5},{5,4},{6,7},{7,6},{8,9},{9,8},{10,11... | collective-permute-start | bytes 3145736 | tf_op jit(solution)/shard_map/ppermute | solution.py:36
  126.8 1.0 copy-start.5
  127.8 0.7 copy-start.23
  132.3 22.4 %all-to-all-start.2 = ((bf16[8,256,256]{2,1,0:T(8,128)(2,1)}), bf16[8,256,256]{2,1,0:T(8,128)(2,1)S(1)}, u32[]{:S(2)}, u32[]{:S(2)}) async-start(bf16[8,256,256]{2,1,0:T(8,128)(2,1)} %shard_map.113), calls=%async_computation.2 | async-start | bytes 2097152 | tf_op jit(solution)/shard_map/all_to_all | solution.py:65
  138.3 1.0 copy-start.4
  141.9 35.7 %copy-start.13 = (f32[1,256,256]{2,1,0:T(8,128)S(1)}, f32[1,256,256]{2,1,0:T(8,128)}, u32[]{:S(2)}) copy-start(f32[1,256,256]{2,1,0:T(8,128)} %param.11) | copy-start | bytes 786436
  141.9 17.8 %collective-permute-start.19 = (bf16[256,256]{1,0:T(8,128)(2,1)}, bf16[256,256]{1,0:T(8,128)(2,1)S(1)}, u32[]{:S(2)}, u32[]{:S(2)}) collective-permute-start(bf16[256,256]{1,0:T(8,128)(2,1)} %get-tuple-element.39), channel_id=1, source_target_pairs={{0,12},{1,28},{2,14},{3,30},{4,8},{5,24},{6,10},{7,26},{8,4},{9,20... | collective-permute-start | bytes 393224 | tf_op jit(solution)/shard_map/ppermute | solution.py:49
  144.9 18.3 %collective-permute-start.20 = (bf16[256,256]{1,0:T(8,128)(2,1)}, bf16[256,256]{1,0:T(8,128)(2,1)S(1)}, u32[]{:S(2)}, u32[]{:S(2)}) collective-permute-start(bf16[256,256]{1,0:T(8,128)(2,1)} %get-tuple-element.40), channel_id=1, source_target_pairs={{0,10},{1,26},{2,12},{3,28},{4,14},{5,30},{6,8},{7,24},{8,2},{9,18... | collective-permute-start | bytes 393224 | tf_op jit(solution)/shard_map/ppermute | solution.py:49
  147.9 16.3 %collective-permute-start.21 = (bf16[256,256]{1,0:T(8,128)(2,1)}, bf16[256,256]{1,0:T(8,128)(2,1)S(1)}, u32[]{:S(2)}, u32[]{:S(2)}) collective-permute-start(bf16[256,256]{1,0:T(8,128)(2,1)} %get-tuple-element.41), channel_id=1, source_target_pairs={{0,14},{1,30},{2,8},{3,24},{4,10},{5,26},{6,12},{7,28},{8,6},{9,22... | collective-permute-start | bytes 393224 | tf_op jit(solution)/shard_map/ppermute | solution.py:49
  154.8 13.2 %copy-start.6 = (bf16[256,256]{1,0:T(8,128)(2,1)}, bf16[256,256]{1,0:T(8,128)(2,1)S(1)}, u32[]{:S(2)}) copy-start(bf16[256,256]{1,0:T(8,128)(2,1)S(1)} %reduce_sum.12.mine) | copy-start | bytes 393220
  154.8 38.7 %copy-start.10 = (f32[1,256,256]{2,1,0:T(8,128)S(1)}, f32[1,256,256]{2,1,0:T(8,128)}, u32[]{:S(2)}) copy-start(f32[1,256,256]{2,1,0:T(8,128)} %param.10) | copy-start | bytes 786436
  154.8 11.6 %collective-permute-start.16 = (bf16[256,256]{1,0:T(8,128)(2,1)S(1)}, bf16[256,256]{1,0:T(8,128)(2,1)S(1)}, u32[]{:S(2)}, u32[]{:S(2)}) collective-permute-start(bf16[256,256]{1,0:T(8,128)(2,1)S(1)} %reduce_sum.12.mine), channel_id=1, source_target_pairs={{0,16},{16,0},{32,48},{48,32},{64,80},{80,64},{96,112},{112,96},{1... | collective-permute-start | bytes 393224 | tf_op jit(solution)/shard_map/ppermute | solution.py:40
  157.1 14.0 %collective-permute-start.22 = (bf16[256,256]{1,0:T(8,128)(2,1)}, bf16[256,256]{1,0:T(8,128)(2,1)S(1)}, u32[]{:S(2)}, u32[]{:S(2)}) collective-permute-start(bf16[256,256]{1,0:T(8,128)(2,1)} %get-tuple-element.42), channel_id=1, source_target_pairs={{0,4},{1,20},{2,6},{3,22},{4,0},{5,16},{6,2},{7,18},{8,12},{9,28},... | collective-permute-start | bytes 393224 | tf_op jit(solution)/shard_map/ppermute | solution.py:49
  159.7 17.3 %collective-permute-start.23 = (bf16[256,256]{1,0:T(8,128)(2,1)}, bf16[256,256]{1,0:T(8,128)(2,1)S(1)}, u32[]{:S(2)}, u32[]{:S(2)}) collective-permute-start(bf16[256,256]{1,0:T(8,128)(2,1)} %get-tuple-element.43), channel_id=1, source_target_pairs={{0,8},{1,24},{2,10},{3,26},{4,12},{5,28},{6,14},{7,30},{8,0},{9,16... | collective-permute-start | bytes 393224 | tf_op jit(solution)/shard_map/ppermute | solution.py:49
  163.2 14.4 %collective-permute-start.24 = (bf16[256,256]{1,0:T(8,128)(2,1)}, bf16[256,256]{1,0:T(8,128)(2,1)S(1)}, u32[]{:S(2)}, u32[]{:S(2)}) collective-permute-start(bf16[256,256]{1,0:T(8,128)(2,1)} %get-tuple-element.44), channel_id=1, source_target_pairs={{0,2},{1,18},{2,4},{3,20},{4,6},{5,22},{6,0},{7,16},{8,10},{9,26},... | collective-permute-start | bytes 393224 | tf_op jit(solution)/shard_map/ppermute | solution.py:49
  164.2 13.5 %collective-permute-start.25 = (bf16[256,256]{1,0:T(8,128)(2,1)}, bf16[256,256]{1,0:T(8,128)(2,1)S(1)}, u32[]{:S(2)}, u32[]{:S(2)}) collective-permute-start(bf16[256,256]{1,0:T(8,128)(2,1)} %get-tuple-element.45), channel_id=1, source_target_pairs={{0,6},{1,22},{2,0},{3,16},{4,2},{5,18},{6,4},{7,20},{8,14},{9,30},... | collective-permute-start | bytes 393224 | tf_op jit(solution)/shard_map/ppermute | solution.py:49
  166.4 1.6 copy-start.21
  166.4 11.2 %collective-permute-start.26 = (bf16[256,256]{1,0:T(8,128)(2,1)}, bf16[256,256]{1,0:T(8,128)(2,1)S(1)}, u32[]{:S(2)}, u32[]{:S(2)}) collective-permute-start(bf16[256,256]{1,0:T(8,128)(2,1)} %get-tuple-element.46), channel_id=1, source_target_pairs={{0,0},{1,16},{2,2},{3,18},{4,4},{5,20},{6,6},{7,22},{8,8},{9,24},{... | collective-permute-start | bytes 393224 | tf_op jit(solution)/shard_map/ppermute | solution.py:49
  171.2 29.0 %copy-start.9 = (f32[256,256]{1,0:T(8,128)S(1)}, f32[256,256]{1,0:T(8,128)}, u32[]{:S(2)}) copy-start(f32[256,256]{1,0:T(8,128)} %get-tuple-element.49) | copy-start | bytes 786436
  171.2 16.8 %collective-permute-start.27 = (bf16[256,256]{1,0:T(8,128)(2,1)}, bf16[256,256]{1,0:T(8,128)(2,1)S(1)}, u32[]{:S(2)}, u32[]{:S(2)}) collective-permute-start(bf16[256,256]{1,0:T(8,128)(2,1)} %get-tuple-element.50), channel_id=1, source_target_pairs={{0,128},{16,144},{32,160},{48,176},{64,192},{80,208},{96,224},{112... | collective-permute-start | bytes 393224 | tf_op jit(solution)/shard_map/ppermute | solution.py:32
  177.0 16.4 %collective-permute-start.28 = (bf16[256,256]{1,0:T(8,128)(2,1)}, bf16[256,256]{1,0:T(8,128)(2,1)S(1)}, u32[]{:S(2)}, u32[]{:S(2)}) collective-permute-start(bf16[256,256]{1,0:T(8,128)(2,1)} %get-tuple-element.51), channel_id=1, source_target_pairs={{0,96},{16,112},{32,128},{48,144},{64,160},{80,176},{96,192},{112,... | collective-permute-start | bytes 393224 | tf_op jit(solution)/shard_map/ppermute | solution.py:32
  178.5 16.6 %collective-permute-start.29 = (bf16[256,256]{1,0:T(8,128)(2,1)}, bf16[256,256]{1,0:T(8,128)(2,1)S(1)}, u32[]{:S(2)}, u32[]{:S(2)}) collective-permute-start(bf16[256,256]{1,0:T(8,128)(2,1)} %get-tuple-element.52), channel_id=1, source_target_pairs={{0,160},{16,176},{32,192},{48,208},{64,224},{80,240},{96,0},{112,1... | collective-permute-start | bytes 393224 | tf_op jit(solution)/shard_map/ppermute | solution.py:32
  182.9 15.0 %collective-permute-start.30 = (bf16[256,256]{1,0:T(8,128)(2,1)}, bf16[256,256]{1,0:T(8,128)(2,1)S(1)}, u32[]{:S(2)}, u32[]{:S(2)}) collective-permute-start(bf16[256,256]{1,0:T(8,128)(2,1)} %get-tuple-element.53), channel_id=1, source_target_pairs={{0,64},{16,80},{32,96},{48,112},{64,128},{80,144},{96,160},{112,17... | collective-permute-start | bytes 393224 | tf_op jit(solution)/shard_map/ppermute | solution.py:32
  183.5 14.6 %collective-permute-start.31 = (bf16[256,256]{1,0:T(8,128)(2,1)}, bf16[256,256]{1,0:T(8,128)(2,1)S(1)}, u32[]{:S(2)}, u32[]{:S(2)}) collective-permute-start(bf16[256,256]{1,0:T(8,128)(2,1)} %get-tuple-element.54), channel_id=1, source_target_pairs={{0,192},{16,208},{32,224},{48,240},{64,0},{80,16},{96,32},{112,48}... | collective-permute-start | bytes 393224 | tf_op jit(solution)/shard_map/ppermute | solution.py:32
  188.0 11.9 %collective-permute-start.32 = (bf16[256,256]{1,0:T(8,128)(2,1)}, bf16[256,256]{1,0:T(8,128)(2,1)S(1)}, u32[]{:S(2)}, u32[]{:S(2)}) collective-permute-start(bf16[256,256]{1,0:T(8,128)(2,1)} %get-tuple-element.55), channel_id=1, source_target_pairs={{0,32},{16,48},{32,64},{48,80},{64,96},{80,112},{96,128},{112,144}... | collective-permute-start | bytes 393224 | tf_op jit(solution)/shard_map/ppermute | solution.py:32
  193.5 6.7 %collective-permute-start.33 = (bf16[256,256]{1,0:T(8,128)(2,1)}, bf16[256,256]{1,0:T(8,128)(2,1)S(1)}, u32[]{:S(2)}, u32[]{:S(2)}) collective-permute-start(bf16[256,256]{1,0:T(8,128)(2,1)} %get-tuple-element.56), channel_id=1, source_target_pairs={{0,224},{16,240},{32,0},{48,16},{64,32},{80,48},{96,64},{112,80},{... | collective-permute-start | bytes 393224 | tf_op jit(solution)/shard_map/ppermute | solution.py:32
Sparse Core Ops, SparseCore 0:
  10.3 43.6 all-gather.1
  114.1 38.9 reduce-scatter.1
